TPU v7x, 32 devices: a whole 2x2x4 slice. The times are simulated.
32 devices in a mesh: dp: 4 (over z), fsdp: 8 (over y, x, core).
Axes of the slice: x: 2, y: 2, z: 4, core: 2. Of those that a mesh axis runs over, the one named last changes fastest.
Arguments:
- tokens: bfloat16 [4096, 1536], P(('dp', 'fsdp')), may hold values from -6 to 6
- segments: int32 [32, 128], P(('dp', 'fsdp')), may hold values from 0 to 3, never falling along the last dimension, each value on 1 to 64 neighbouring positions
- cotangent: bfloat16 [4096, 1536], P(('dp', 'fsdp')), may hold values from -6 to 6
- norm_gains: bfloat16 [2, 1536], P(None, ('dp', 'fsdp')), may hold values from 0.5 to 1.5
- w_query: bfloat16 [1536, 1536], P(('dp', 'fsdp')), may hold values from -0.15625 to 0.15625
- w_key: bfloat16 [1536, 768], P(('dp', 'fsdp')), may hold values from -0.15625 to 0.15625
- w_value: bfloat16 [1536, 768], P(('dp', 'fsdp')), may hold values from -0.15625 to 0.15625
- w_out: bfloat16 [1536, 1536], P(('dp', 'fsdp')), may hold values from -0.875 to 0.875
- w_gate: bfloat16 [1536, 4096], P(('dp', 'fsdp')), may hold values from -0.15625 to 0.15625
- w_up: bfloat16 [1536, 4096], P(('dp', 'fsdp')), may hold values from -0.15625 to 0.15625
- w_down: bfloat16 [4096, 1536], P(('dp', 'fsdp')), may hold values from -0.09375 to 0.09375
- moment_gains: float32 [2, 1536], P(None, ('dp', 'fsdp')), may hold values from -128 to 128
- moment_query: float32 [1536, 1536], P(('dp', 'fsdp')), may hold values from -128 to 128
- moment_key: float32 [1536, 768], P(('dp', 'fsdp')), may hold values from -128 to 128
- moment_value: float32 [1536, 768], P(('dp', 'fsdp')), may hold values from -256 to 256
- moment_out: float32 [1536, 1536], P(('dp', 'fsdp')), may hold values from -32 to 32
- moment_gate: float32 [1536, 4096], P(('dp', 'fsdp')), may hold values from -32 to 32
- moment_up: float32 [1536, 4096], P(('dp', 'fsdp')), may hold values from -32 to 32
- moment_down: float32 [4096, 1536], P(('dp', 'fsdp')), may hold values from -32 to 32
Outputs:
- outputs: bfloat16 [4096, 1536], P(('dp', 'fsdp'))
- grad_tokens: float32 [4096, 1536], P(('dp', 'fsdp'))
- grad_gains: float32 [2, 1536], P(None, ('dp', 'fsdp'))
- grad_query: float32 [1536, 1536], P(('dp', 'fsdp'))
- grad_key: float32 [1536, 768], P(('dp', 'fsdp'))
- grad_value: float32 [1536, 768], P(('dp', 'fsdp'))
- grad_out: float32 [1536, 1536], P(('dp', 'fsdp'))
- grad_gate: float32 [1536, 4096], P(('dp', 'fsdp'))
- grad_up: float32 [1536, 4096], P(('dp', 'fsdp'))
- grad_down: float32 [4096, 1536], P(('dp', 'fsdp'))
- update_gains: float32 [2, 1536], P(None, ('dp', 'fsdp'))
- update_query: float32 [1536, 1536], P(('dp', 'fsdp'))
- update_key: float32 [1536, 768], P(('dp', 'fsdp'))
- update_value: float32 [1536, 768], P(('dp', 'fsdp'))
- update_out: float32 [1536, 1536], P(('dp', 'fsdp'))
- update_gate: float32 [1536, 4096], P(('dp', 'fsdp'))
- update_up: float32 [1536, 4096], P(('dp', 'fsdp'))
- update_down: float32 [4096, 1536], P(('dp', 'fsdp'))
- new_moment_gains: float32 [2, 1536], P(None, ('dp', 'fsdp'))
- new_moment_query: float32 [1536, 1536], P(('dp', 'fsdp'))
- new_moment_key: float32 [1536, 768], P(('dp', 'fsdp'))
- new_moment_value: float32 [1536, 768], P(('dp', 'fsdp'))
- new_moment_out: float32 [1536, 1536], P(('dp', 'fsdp'))
- new_moment_gate: float32 [1536, 4096], P(('dp', 'fsdp'))
- new_moment_up: float32 [1536, 4096], P(('dp', 'fsdp'))
- new_moment_down: float32 [4096, 1536], P(('dp', 'fsdp'))
Inputs may be any that keep to these rules, and one draw needn't show every extreme that they name: `segments`: within each sequence the document numbers never fall; each document holds 1 to 64 tokens.
All inputs are finite; a program needn't handle non-finite values.
Results may differ from a plain program's by a relative error of at most 0.025.
Values may be sent and summed in bfloat16 or wider, within the bound.
A program may use at most 320 MiB of HBM per device.

v0:
```python
import math

import jax
import jax.numpy as jnp
from jax import lax
from jax.sharding import PartitionSpec as P

D = 1536
HEADS = 16
KV_HEADS = 8
HEAD_DIM = 96
FF = 4096
NS_STEPS = 3
KVW = 768


eps_norm = 1e-05
rope_base = 100000.0
coeff_a = 3.4445
coeff_b = -4.775
coeff_c = 2.0315
beta_moment = 0.95
rate_matrix = 0.2
rate_gain = 0.05
masked_score = -1e30


def rope_tables(length, head_width):
    half_width = head_width // 2
    frequency = rope_base ** (-(jnp.arange(half_width, dtype=jnp.float32) * 2.0 / head_width))
    angles = jnp.arange(length, dtype=jnp.float32)[:, None] * frequency[None, :]
    return (jnp.cos(angles)[:, None, :], jnp.sin(angles)[:, None, :])


def rotate(head_rows, cosine, sine_table):
    half_width = head_rows.shape[-1] // 2
    leading = head_rows[..., :half_width]
    trailing = head_rows[..., half_width:]
    return jnp.concatenate(
        [leading * cosine - trailing * sine_table, trailing * cosine + leading * sine_table],
        axis=-1,
    )


def unrotate(grad_rows, cosine, sine_table):
    half_width = grad_rows.shape[-1] // 2
    leading = grad_rows[..., :half_width]
    trailing = grad_rows[..., half_width:]
    return jnp.concatenate(
        [leading * cosine + trailing * sine_table, trailing * cosine - leading * sine_table],
        axis=-1,
    )


def rms_inverse(activation):
    return lax.rsqrt(jnp.mean(activation * activation, axis=-1, keepdims=True) + eps_norm)


def rms_back(grad_normed, normed, inverse):
    return inverse * (grad_normed - normed * jnp.mean(grad_normed * normed, axis=-1, keepdims=True))


def score_block(query_rot, key_rot, allowed):
    score_scale = 1.0 / math.sqrt(HEAD_DIM)
    raw_scores = jnp.einsum(
        "qhgd,khd->hgqk", query_rot, key_rot, preferred_element_type=jnp.float32
    )
    return jnp.where(allowed, raw_scores * score_scale, masked_score)


def newton_padded(oriented_low):
    as_float = oriented_low.astype(jnp.float32)
    frobenius = jnp.sqrt(jnp.sum(as_float * as_float))
    iterate = (as_float / (frobenius + 1e-07)).astype(jnp.bfloat16)
    for number in range(NS_STEPS):
        gram_low = jnp.einsum(
            "ik,jk->ij", iterate, iterate, preferred_element_type=jnp.float32
        ).astype(jnp.bfloat16)
        square = jnp.dot(gram_low, gram_low, preferred_element_type=jnp.float32)
        mixer = (coeff_b * gram_low.astype(jnp.float32) + coeff_c * square).astype(jnp.bfloat16)
        product = jnp.dot(mixer, iterate, preferred_element_type=jnp.float32)
        iterate = (coeff_a * iterate.astype(jnp.float32) + product).astype(jnp.bfloat16)
    return iterate


def body(
    tokens,
    segments,
    cotangent,
    norm_gains,
    w_query,
    w_key,
    w_value,
    w_out,
    w_gate,
    w_up,
    w_down,
    moment_gains,
    moment_query,
    moment_key,
    moment_value,
    moment_out,
    moment_gate,
    moment_up,
    moment_down,
):
    gathered = (
        lax.all_gather(norm_gains, ("dp", "fsdp"), axis=1, tiled=True),
        lax.all_gather(w_query, ("dp", "fsdp"), axis=0, tiled=True),
        lax.all_gather(w_key, ("dp", "fsdp"), axis=0, tiled=True),
        lax.all_gather(w_value, ("dp", "fsdp"), axis=0, tiled=True),
        lax.all_gather(w_out, ("dp", "fsdp"), axis=0, tiled=True),
        lax.all_gather(w_gate, ("dp", "fsdp"), axis=0, tiled=True),
        lax.all_gather(w_up, ("dp", "fsdp"), axis=0, tiled=True),
        lax.all_gather(w_down, ("dp", "fsdp"), axis=0, tiled=True),
    )
    gains_full, query_full, key_full, value_full, out_full, gate_full, up_full, down_full = gathered
    length = tokens.shape[0]
    group_size = HEADS // KV_HEADS
    cosine, sine_table = rope_tables(length, HEAD_DIM)
    segment_row = segments[0]
    positions = jnp.arange(length)
    allowed = (segment_row[:, None] == segment_row[None, :]) & (
        positions[None, :] <= positions[:, None]
    )
    residual_in = tokens.astype(jnp.float32)
    gain_rows = gains_full.astype(jnp.float32)
    inverse_one = rms_inverse(residual_in)
    normed_one = residual_in * inverse_one
    entry_one = (normed_one * gain_rows[0]).astype(jnp.bfloat16)
    query_pre = jnp.dot(entry_one, query_full, preferred_element_type=jnp.float32)
    key_pre = jnp.dot(entry_one, key_full, preferred_element_type=jnp.float32)
    values = jnp.dot(entry_one, value_full, preferred_element_type=jnp.float32).astype(jnp.bfloat16)
    query_rot = rotate(query_pre.reshape(length, HEADS, HEAD_DIM), cosine, sine_table).astype(
        jnp.bfloat16
    )
    query_rot = query_rot.reshape(length, KV_HEADS, group_size, HEAD_DIM)
    key_rot = rotate(key_pre.reshape(length, KV_HEADS, HEAD_DIM), cosine, sine_table).astype(
        jnp.bfloat16
    )
    value_heads = values.reshape(length, KV_HEADS, HEAD_DIM)
    scores = score_block(query_rot, key_rot, allowed)
    row_max = jnp.max(scores, axis=-1, keepdims=True)
    log_total = row_max + jnp.log(jnp.sum(jnp.exp(scores - row_max), axis=-1, keepdims=True))
    attention_low = jnp.exp(scores - log_total).astype(jnp.bfloat16)
    attn_low = (
        jnp.einsum("hgqk,khd->qhgd", attention_low, value_heads, preferred_element_type=jnp.float32)
        .reshape(length, D)
        .astype(jnp.bfloat16)
    )
    hidden = residual_in + jnp.dot(attn_low, out_full, preferred_element_type=jnp.float32)
    inverse_two = rms_inverse(hidden)
    normed_two = hidden * inverse_two
    entry_two = (normed_two * gain_rows[1]).astype(jnp.bfloat16)
    gate_pre = jnp.dot(entry_two, gate_full, preferred_element_type=jnp.float32)
    up_pre = jnp.dot(entry_two, up_full, preferred_element_type=jnp.float32)
    gate_sig = jax.nn.sigmoid(gate_pre)
    act_low = (gate_pre * gate_sig * up_pre).astype(jnp.bfloat16)
    down_out = jnp.dot(act_low, down_full, preferred_element_type=jnp.float32)
    outputs = (hidden + down_out).astype(jnp.bfloat16)
    regathered = (
        lax.all_gather(norm_gains, ("dp", "fsdp"), axis=1, tiled=True),
        lax.all_gather(w_query, ("dp", "fsdp"), axis=0, tiled=True),
        lax.all_gather(w_key, ("dp", "fsdp"), axis=0, tiled=True),
        lax.all_gather(w_value, ("dp", "fsdp"), axis=0, tiled=True),
        lax.all_gather(w_out, ("dp", "fsdp"), axis=0, tiled=True),
        lax.all_gather(w_gate, ("dp", "fsdp"), axis=0, tiled=True),
        lax.all_gather(w_up, ("dp", "fsdp"), axis=0, tiled=True),
        lax.all_gather(w_down, ("dp", "fsdp"), axis=0, tiled=True),
    )
    gains_back, query_back, key_back, value_back, out_back, gate_back, up_back, down_back = (
        regathered
    )
    back_rows = gains_back.astype(jnp.float32)
    cot_float = cotangent.astype(jnp.float32)
    d_act = jnp.einsum("td,fd->tf", cotangent, down_back, preferred_element_type=jnp.float32)
    d_gate_low = (d_act * up_pre * gate_sig * (1.0 + gate_pre * (1.0 - gate_sig))).astype(
        jnp.bfloat16
    )
    d_up_low = (d_act * gate_pre * gate_sig).astype(jnp.bfloat16)
    fsdp_count = lax.axis_size("fsdp")
    dp_count = lax.axis_size("dp")
    row_share = D // (fsdp_count * dp_count)
    ff_share = FF // (fsdp_count * dp_count)
    entry_split = entry_two.reshape(length, dp_count, fsdp_count, row_share)
    act_split = act_low.reshape(length, dp_count, fsdp_count, ff_share)
    entry_cols, act_cols = (
        lax.all_to_all(entry_split, "fsdp", split_axis=2, concat_axis=0, tiled=True),
        lax.all_to_all(act_split, "fsdp", split_axis=2, concat_axis=0, tiled=True),
    )
    entry_cols = entry_cols.reshape(fsdp_count * length, dp_count * row_share)
    act_cols = act_cols.reshape(fsdp_count * length, dp_count * ff_share)
    gate_group, up_group, cot_group = (
        lax.all_gather(d_gate_low, "fsdp", axis=0, tiled=True),
        lax.all_gather(d_up_low, "fsdp", axis=0, tiled=True),
        lax.all_gather(cotangent, "fsdp", axis=0, tiled=True),
    )
    gate_part = jnp.einsum("td,tf->df", entry_cols, gate_group, preferred_element_type=jnp.float32)
    up_part = jnp.einsum("td,tf->df", entry_cols, up_group, preferred_element_type=jnp.float32)
    down_part = jnp.einsum("tf,td->fd", act_cols, cot_group, preferred_element_type=jnp.float32)
    ffn_summed = (
        lax.psum_scatter(
            gate_part.astype(jnp.bfloat16), "dp", scatter_dimension=0, tiled=True
        ).astype(jnp.float32),
        lax.psum_scatter(
            up_part.astype(jnp.bfloat16), "dp", scatter_dimension=0, tiled=True
        ).astype(jnp.float32),
        lax.psum_scatter(
            down_part.astype(jnp.bfloat16), "dp", scatter_dimension=0, tiled=True
        ).astype(jnp.float32),
    )
    d_entry_two = jnp.einsum(
        "tf,df->td", d_gate_low, gate_back, preferred_element_type=jnp.float32
    ) + jnp.einsum("tf,df->td", d_up_low, up_back, preferred_element_type=jnp.float32)
    d_hidden = cot_float + rms_back(d_entry_two * back_rows[1], normed_two, inverse_two)
    d_hidden_low = d_hidden.astype(jnp.bfloat16)
    grad_out = jnp.einsum("td,te->de", attn_low, d_hidden_low, preferred_element_type=jnp.float32)
    d_attn = jnp.einsum("te,de->td", d_hidden_low, out_back, preferred_element_type=jnp.float32)
    d_attn = d_attn.astype(jnp.bfloat16).reshape(length, KV_HEADS, group_size, HEAD_DIM)
    scores_again = score_block(query_rot, key_rot, allowed)
    attention = jnp.exp(scores_again - log_total)
    attention_again = attention.astype(jnp.bfloat16)
    d_probs = jnp.einsum("qhgd,khd->hgqk", d_attn, value_heads, preferred_element_type=jnp.float32)
    d_values = jnp.einsum(
        "hgqk,qhgd->khd", attention_again, d_attn, preferred_element_type=jnp.float32
    )
    d_values = d_values.reshape(length, KVW).astype(jnp.bfloat16)
    row_delta = jnp.sum(attention * d_probs, axis=-1, keepdims=True)
    d_scores = (attention * (d_probs - row_delta)).astype(jnp.bfloat16)
    score_scale = 1.0 / math.sqrt(HEAD_DIM)
    d_query_rot = (
        jnp.einsum("hgqk,khd->qhgd", d_scores, key_rot, preferred_element_type=jnp.float32)
        * score_scale
    )
    d_key_rot = (
        jnp.einsum("hgqk,qhgd->khd", d_scores, query_rot, preferred_element_type=jnp.float32)
        * score_scale
    )
    d_query = unrotate(d_query_rot.reshape(length, HEADS, HEAD_DIM), cosine, sine_table)
    d_query = d_query.reshape(length, D).astype(jnp.bfloat16)
    d_key = unrotate(d_key_rot, cosine, sine_table).reshape(length, KVW).astype(jnp.bfloat16)
    grad_query = jnp.einsum("td,te->de", entry_one, d_query, preferred_element_type=jnp.float32)
    grad_key = jnp.einsum("td,te->de", entry_one, d_key, preferred_element_type=jnp.float32)
    grad_value = jnp.einsum("td,te->de", entry_one, d_values, preferred_element_type=jnp.float32)
    d_entry_one = (
        jnp.einsum("te,de->td", d_query, query_back, preferred_element_type=jnp.float32)
        + jnp.einsum("te,de->td", d_key, key_back, preferred_element_type=jnp.float32)
        + jnp.einsum("te,de->td", d_values, value_back, preferred_element_type=jnp.float32)
    )
    grad_gain_rows = jnp.stack(
        [jnp.sum(d_entry_one * normed_one, axis=0), jnp.sum(d_entry_two * normed_two, axis=0)]
    )
    grad_tokens = d_hidden + rms_back(d_entry_one * back_rows[0], normed_one, inverse_one)
    attn_summed = (
        lax.psum_scatter(grad_gain_rows, ("dp", "fsdp"), scatter_dimension=1, tiled=True),
        lax.psum_scatter(grad_query, ("dp", "fsdp"), scatter_dimension=0, tiled=True),
        lax.psum_scatter(grad_key, ("dp", "fsdp"), scatter_dimension=0, tiled=True),
        lax.psum_scatter(grad_value, ("dp", "fsdp"), scatter_dimension=0, tiled=True),
        lax.psum_scatter(grad_out, ("dp", "fsdp"), scatter_dimension=0, tiled=True),
    )
    summed = (
        attn_summed[0],
        attn_summed[1],
        attn_summed[2],
        attn_summed[3],
        attn_summed[4],
        ffn_summed[0],
        ffn_summed[1],
        ffn_summed[2],
    )
    moments_old = (
        moment_gains,
        moment_query,
        moment_key,
        moment_value,
        moment_out,
        moment_gate,
        moment_up,
        moment_down,
    )
    new_moments = tuple(
        (
            beta_moment * old_moment + grad_shard
            for old_moment, grad_shard in zip(moments_old, summed)
        )
    )
    nesterov = tuple(
        (
            (grad_shard + beta_moment * moment_now).astype(jnp.bfloat16)
            for grad_shard, moment_now in zip(summed, new_moments)
        )
    )
    device = lax.axis_index(("dp", "fsdp"))
    dev_count = lax.axis_size(("dp", "fsdp"))
    whole_shapes = [
        (nesterov[slot].shape[0] * dev_count, nesterov[slot].shape[1]) for slot in range(1, 8)
    ]
    shard_sizes = [nesterov[slot].shape[0] * nesterov[slot].shape[1] for slot in range(1, 8)]
    piece_width = max(shard_sizes)
    received = (
        lax.all_gather(nesterov[0], ("dp", "fsdp"), axis=1, tiled=True),
        lax.all_gather(nesterov[1], ("dp", "fsdp"), axis=0, tiled=True),
        lax.all_gather(nesterov[2], ("dp", "fsdp"), axis=0, tiled=True),
        lax.all_gather(nesterov[3], ("dp", "fsdp"), axis=0, tiled=True),
        lax.all_gather(nesterov[4], ("dp", "fsdp"), axis=0, tiled=True),
        lax.all_gather(nesterov[5], ("dp", "fsdp"), axis=0, tiled=True),
        lax.all_gather(nesterov[6], ("dp", "fsdp"), axis=0, tiled=True),
        lax.all_gather(nesterov[7], ("dp", "fsdp"), axis=0, tiled=True),
    )
    gain_whole = received[0]
    whole_dirs = [received[slot] for slot in range(1, 8)]
    gain_dir = gain_whole.astype(jnp.float32)
    gain_step = (
        -rate_gain
        * gain_dir
        * lax.rsqrt(jnp.mean(gain_dir * gain_dir, axis=-1, keepdims=True) + 1e-06)
    )
    gain_width = norm_gains.shape[1]
    update_gains = lax.dynamic_slice_in_dim(gain_step, device * gain_width, gain_width, 1)
    padded_list = []
    flip_list = []
    for owner_id in range(7):
        matrix_low = whole_dirs[owner_id]
        flipped = matrix_low.shape[0] > matrix_low.shape[1]
        oriented = matrix_low.T if flipped else matrix_low
        flip_list.append(flipped)
        padded_list.append(
            jnp.pad(oriented, ((0, D - oriented.shape[0]), (0, FF - oriented.shape[1])))
        )
    stacked = jnp.stack(padded_list)
    own_dir = lax.dynamic_index_in_dim(stacked, jnp.minimum(device, 6), 0, keepdims=False)
    own_result = newton_padded(own_dir)
    orthogonal = []
    for owner_id in range(7):
        row_count, col_count = whole_shapes[owner_id]
        short_side = min(row_count, col_count)
        long_side = max(row_count, col_count)
        piece = own_result[:short_side, :long_side]
        piece = piece.T if flip_list[owner_id] else piece
        orthogonal.append(jnp.where(device == owner_id, piece, jnp.zeros_like(piece)))
    outgoing_blocks = jnp.zeros((dev_count, piece_width), jnp.bfloat16)
    for owner_id in range(7):
        block_rows = orthogonal[owner_id].reshape(dev_count, shard_sizes[owner_id])
        outgoing_blocks = outgoing_blocks + jnp.pad(
            block_rows, ((0, 0), (0, piece_width - shard_sizes[owner_id]))
        )
    incoming_blocks = lax.all_to_all(
        outgoing_blocks, ("dp", "fsdp"), split_axis=0, concat_axis=0, tiled=True
    )
    shards = []
    for owner_id in range(7):
        shard_shape = nesterov[owner_id + 1].shape
        shards.append(
            incoming_blocks[owner_id, : shard_sizes[owner_id]]
            .reshape(shard_shape)
            .astype(jnp.float32)
        )
    updates = [update_gains]
    for owner_id in range(7):
        row_count, col_count = whole_shapes[owner_id]
        factor = math.sqrt(max(1.0, col_count / row_count))
        updates.append(-rate_matrix * factor * shards[owner_id])
    return (
        outputs,
        grad_tokens,
        summed[0],
        summed[1],
        summed[2],
        summed[3],
        summed[4],
        summed[5],
        summed[6],
        summed[7],
        updates[0],
        updates[1],
        updates[2],
        updates[3],
        updates[4],
        updates[5],
        updates[6],
        updates[7],
        new_moments[0],
        new_moments[1],
        new_moments[2],
        new_moments[3],
        new_moments[4],
        new_moments[5],
        new_moments[6],
        new_moments[7],
    )


def solution(mesh):
    return jax.shard_map(
        body,
        mesh=mesh,
        in_specs=(
            P(("dp", "fsdp"), None),
            P(("dp", "fsdp"), None),
            P(("dp", "fsdp"), None),
            P(None, ("dp", "fsdp")),
            P(("dp", "fsdp"), None),
            P(("dp", "fsdp"), None),
            P(("dp", "fsdp"), None),
            P(("dp", "fsdp"), None),
            P(("dp", "fsdp"), None),
            P(("dp", "fsdp"), None),
            P(("dp", "fsdp"), None),
            P(None, ("dp", "fsdp")),
            P(("dp", "fsdp"), None),
            P(("dp", "fsdp"), None),
            P(("dp", "fsdp"), None),
            P(("dp", "fsdp"), None),
            P(("dp", "fsdp"), None),
            P(("dp", "fsdp"), None),
            P(("dp", "fsdp"), None),
        ),
        out_specs=(
            P(("dp", "fsdp"), None),
            P(("dp", "fsdp"), None),
            P(None, ("dp", "fsdp")),
            P(("dp", "fsdp"), None),
            P(("dp", "fsdp"), None),
            P(("dp", "fsdp"), None),
            P(("dp", "fsdp"), None),
            P(("dp", "fsdp"), None),
            P(("dp", "fsdp"), None),
            P(("dp", "fsdp"), None),
            P(None, ("dp", "fsdp")),
            P(("dp", "fsdp"), None),
            P(("dp", "fsdp"), None),
            P(("dp", "fsdp"), None),
            P(("dp", "fsdp"), None),
            P(("dp", "fsdp"), None),
            P(("dp", "fsdp"), None),
            P(("dp", "fsdp"), None),
            P(None, ("dp", "fsdp")),
            P(("dp", "fsdp"), None),
            P(("dp", "fsdp"), None),
            P(("dp", "fsdp"), None),
            P(("dp", "fsdp"), None),
            P(("dp", "fsdp"), None),
            P(("dp", "fsdp"), None),
            P(("dp", "fsdp"), None),
        ),
        check_vma=False,
    )
```

profile of v0, /device:TPU:14, one launch (start us, length us, event | category | flops | bytes accessed | tf_op | source)
XLA Modules:
  0.0 2655.6 jit_solution(14655385675335945807)
XLA Ops:
  69.8 56.2 %all-gather.22.cloned.1.call-done = bf16[1536,768]{1,0:T(8,128)(2,1)} async-done(((bf16[48,768]{1,0:T(8,128)(2,1)}), bf16[1536,768]{1,0:T(8,128)(2,1)}) %all-gather.22.cloned.1.call-update) | async-done | bytes 2359312 | tf_op jit(solution)/shard_map/all_gather | solution.py:110
  129.1 63.1 %all-gather.24.cloned.1.call-done = bf16[1536,1536]{1,0:T(8,128)(2,1)} async-done(((bf16[48,1536]{1,0:T(8,128)(2,1)}), bf16[1536,1536]{1,0:T(8,128)(2,1)}) %all-gather.24.cloned.1.call-update) | async-done | bytes 4718608 | tf_op jit(solution)/shard_map/all_gather | solution.py:109
  197.5 59.3 %all-gather.26.cloned.1.call-done = bf16[1536,1536]{1,0:T(8,128)(2,1)} async-done(((bf16[48,1536]{1,0:T(8,128)(2,1)}), bf16[1536,1536]{1,0:T(8,128)(2,1)}) %all-gather.26.cloned.1.call-update) | async-done | bytes 4718608 | tf_op jit(solution)/shard_map/all_gather | solution.py:112
  261.1 91.8 %all-gather.28.cloned.1.call-done = bf16[1536,4096]{1,0:T(8,128)(2,1)} async-done(((bf16[48,4096]{1,0:T(8,128)(2,1)}), bf16[1536,4096]{1,0:T(8,128)(2,1)}) %all-gather.28.cloned.1.call-update) | async-done | bytes 12582928 | tf_op jit(solution)/shard_map/all_gather | solution.py:113
  360.6 88.8 %all-gather.30.cloned.1.call-done = bf16[1536,4096]{1,0:T(8,128)(2,1)} async-done(((bf16[48,4096]{1,0:T(8,128)(2,1)}), bf16[1536,4096]{1,0:T(8,128)(2,1)}) %all-gather.30.cloned.1.call-update) | async-done | bytes 12582928 | tf_op jit(solution)/shard_map/all_gather | solution.py:114
  457.2 88.8 %all-gather.32.cloned.1.call-done = bf16[4096,1536]{1,0:T(8,128)(2,1)} async-done(((bf16[128,1536]{1,0:T(8,128)(2,1)}), bf16[4096,1536]{1,0:T(8,128)(2,1)}) %all-gather.32.cloned.1.call-update) | async-done | bytes 12582928 | tf_op jit(solution)/shard_map/all_gather | solution.py:115
  626.4 41.1 %all-gather.36.cloned.1.call-done = bf16[1024,4096]{1,0:T(8,128)(2,1)} async-done(((bf16[128,4096]{1,0:T(8,128)(2,1)}), bf16[1024,4096]{1,0:T(8,128)(2,1)}) %all-gather.36.cloned.1.call-update) | async-done | bytes 8388624 | tf_op jit(solution)/shard_map/all_gather | solution.py:195
  712.9 109.1 %reduce-scatter.27.cloned.1.call-done = f32[48,768]{1,0:T(8,128)} async-done(((f32[1536,768]{1,0:T(8,128)}), f32[48,768]{1,0:T(8,128)}) %reduce-scatter.27.cloned.1.call-update) | async-done | bytes 147472
  823.8 110.7 %reduce-scatter.29.cloned.1.call-done = f32[48,768]{1,0:T(8,128)} async-done(((f32[1536,768]{1,0:T(8,128)}), f32[48,768]{1,0:T(8,128)}) %reduce-scatter.29.cloned.1.call-update) | async-done | bytes 147472
  936.2 139.9 %reduce-scatter.17.cloned.1.call-done = f32[48,1536]{1,0:T(8,128)} async-done(((f32[1536,1536]{1,0:T(8,128)}), f32[48,1536]{1,0:T(8,128)}) %reduce-scatter.17.cloned.1.call-update) | async-done | bytes 294928 | tf_op jit(solution)/shard_map/reduce_scatter | solution.py:256
  1078.1 139.5 %reduce-scatter.19.cloned.1.call-done = f32[48,1536]{1,0:T(8,128)} async-done(((f32[1536,1536]{1,0:T(8,128)}), f32[48,1536]{1,0:T(8,128)}) %reduce-scatter.19.cloned.1.call-update) | async-done | bytes 294928 | tf_op jit(solution)/shard_map/reduce_scatter | solution.py:259
  1219.5 33.7 %reduce-scatter.21.cloned.1.call-done = bf16[48,4096]{1,0:T(8,128)(2,1)} async-done(((bf16[192,4096]{1,0:T(8,128)(2,1)}), bf16[48,4096]{1,0:T(8,128)(2,1)}) %reduce-scatter.21.cloned.1.call-update) | async-done | bytes 393232 | tf_op jit(solution)/shard_map/reduce_scatter | solution.py:202
  1255.8 33.9 %reduce-scatter.23.cloned.1.call-done = bf16[48,4096]{1,0:T(8,128)(2,1)} async-done(((bf16[192,4096]{1,0:T(8,128)(2,1)}), bf16[48,4096]{1,0:T(8,128)(2,1)}) %reduce-scatter.23.cloned.1.call-update) | async-done | bytes 393232 | tf_op jit(solution)/shard_map/reduce_scatter | solution.py:205
  1292.7 33.5 %reduce-scatter.31.cloned.1.call-done = bf16[128,1536]{1,0:T(8,128)(2,1)} async-done(((bf16[512,1536]{1,0:T(8,128)(2,1)}), bf16[128,1536]{1,0:T(8,128)(2,1)}) %reduce-scatter.31.cloned.1.call-update) | async-done | bytes 393232
  1328.6 55.8 %all-gather.42.cloned.1.call-done = bf16[1536,768]{1,0:T(8,128)(2,1)} async-done(((bf16[48,768]{1,0:T(8,128)(2,1)}), bf16[1536,768]{1,0:T(8,128)(2,1)}) %all-gather.42.cloned.1.call-update) | async-done | bytes 2359312 | tf_op jit(solution)/shard_map/all_gather | solution.py:303
  1387.3 55.9 %all-gather.44.cloned.1.call-done = bf16[1536,768]{1,0:T(8,128)(2,1)} async-done(((bf16[48,768]{1,0:T(8,128)(2,1)}), bf16[1536,768]{1,0:T(8,128)(2,1)}) %all-gather.44.cloned.1.call-update) | async-done | bytes 2359312 | tf_op jit(solution)/shard_map/all_gather | solution.py:304
  1447.5 62.1 %all-gather.40.cloned.1.call-done = bf16[1536,1536]{1,0:T(8,128)(2,1)} async-done(((bf16[48,1536]{1,0:T(8,128)(2,1)}), bf16[1536,1536]{1,0:T(8,128)(2,1)}) %all-gather.40.cloned.1.call-update) | async-done | bytes 4718608 | tf_op jit(solution)/shard_map/all_gather | solution.py:302
  1532.3 42.8 %all-gather.46.cloned.1.call-done = bf16[1536,1536]{1,0:T(8,128)(2,1)} async-done(((bf16[48,1536]{1,0:T(8,128)(2,1)}), bf16[1536,1536]{1,0:T(8,128)(2,1)}) %all-gather.46.cloned.1.call-update) | async-done | bytes 4718608 | tf_op jit(solution)/shard_map/all_gather | solution.py:305
  1583.7 88.2 %all-gather.48.cloned.1.call-done = bf16[1536,4096]{1,0:T(8,128)(2,1)} async-done(((bf16[48,4096]{1,0:T(8,128)(2,1)}), bf16[1536,4096]{1,0:T(8,128)(2,1)}) %all-gather.48.cloned.1.call-update) | async-done | bytes 12582928 | tf_op jit(solution)/shard_map/all_gather | solution.py:306
  1682.5 86.6 %all-gather.50.cloned.1.call-done = bf16[1536,4096]{1,0:T(8,128)(2,1)} async-done(((bf16[48,4096]{1,0:T(8,128)(2,1)}), bf16[1536,4096]{1,0:T(8,128)(2,1)}) %all-gather.50.cloned.1.call-update) | async-done | bytes 12582928 | tf_op jit(solution)/shard_map/all_gather | solution.py:307
  1779.7 108.7 %all-gather.52.cloned.1.call-done = bf16[4096,1536]{0,1:T(8,128)(2,1)} async-done(((bf16[128,1536]{0,1:T(8,128)(2,1)}), bf16[4096,1536]{0,1:T(8,128)(2,1)}) %all-gather.52.cloned.1.call-update) | async-done | bytes 12582928 | tf_op jit(solution)/shard_map/all_gather | solution.py:308
  1948.9 30.9 %add_convert_fusion.2 = bf16[1536,4096]{1,0:T(8,128)(2,1)} fusion(f32[]{:T(128)S(6)} %add.236, bf16[7,1536,4096]{2,1,0:T(8,128)(2,1)} %bitcast_dynamic-update-slice_fusion, s32[]{:T(128)S(6)} %select_n.74, bf16[1536,1536]{1,0:T(8,128)(2,1)} %add_convert_fusion.5.clone.5), kind=kOutput, calls=%fused_computation.6 | convolution fusion | flops 19390267392 | bytes 42469376 | tf_op jit(solution)/shard_map/dot_general | solution.py:81
  2295.0 144.1 %reduce-scatter.25.cloned.1.call-done = f32[48,2]{1,0:T(8,128)} async-done(((f32[1536,2]{1,0:T(8,128)}), f32[48,2]{1,0:T(8,128)}) %reduce-scatter.25.cloned.1.call-update) | async-done | bytes 400
  2440.5 137.3 %all-gather.1 = bf16[32,48,2]{1,2,0:T(2,128)(2,1)S(1)} all-gather(bf16[1,48,2]{1,2,0:T(2,128)(2,1)S(1)} %get-tuple-element.183), channel_id=1, replica_groups=mesh['dp'=4,'fsdp'=8] {'dp','fsdp'}, dimensions={0}, use_global_device_ids=true | all-gather | bytes 6336 | tf_op jit(solution)/shard_map/all_gather | solution.py:301
  (267 shorter events, 737.8 us)
Async XLA Ops:
  7.9 118.1 %all-gather.22.cloned.1.call-start = ((), (), s32[]{:S(2)}) async-start(), calls=%async_computation.12 | async-start | bytes 2433024 | tf_op jit(solution)/shard_map/all_gather | solution.py:110
  8.7 183.4 %all-gather.24.cloned.1.call-start = ((), (), s32[]{:S(2)}) async-start(), calls=%async_computation.13 | async-start | bytes 4866048 | tf_op jit(solution)/shard_map/all_gather | solution.py:109
  9.4 247.4 %all-gather.26.cloned.1.call-start = ((), (), s32[]{:S(2)}) async-start(), calls=%async_computation.14 | async-start | bytes 4866048 | tf_op jit(solution)/shard_map/all_gather | solution.py:112
  10.0 342.9 %all-gather.28.cloned.1.call-start = ((), (), s32[]{:S(2)}) async-start(), calls=%async_computation.15 | async-start | bytes 12976128 | tf_op jit(solution)/shard_map/all_gather | solution.py:113
  10.6 438.8 %all-gather.30.cloned.1.call-start = ((), (), s32[]{:S(2)}) async-start(), calls=%async_computation.16 | async-start | bytes 12976128 | tf_op jit(solution)/shard_map/all_gather | solution.py:114
  11.2 534.9 %all-gather.32.cloned.1.call-start = ((), (), s32[]{:S(2)}) async-start(), calls=%async_computation.17 | async-start | bytes 12976128 | tf_op jit(solution)/shard_map/all_gather | solution.py:115
  11.9 607.3 %all-gather.34.cloned.1.call-start = ((), (), s32[]{:S(2)}) async-start(), calls=%async_computation.20 | async-start | bytes 9437184 | tf_op jit(solution)/shard_map/all_gather | solution.py:194
  558.7 149.1 %all-gather.38.cloned.1.call-start = ((), (), s32[]{:S(2)}) async-start(), calls=%async_computation.24 | async-start | bytes 3538944 | tf_op jit(solution)/shard_map/all_gather | solution.py:196
  559.3 262.7 %reduce-scatter.27.cloned.1.call-start = ((), (), s32[]{:S(2)}) async-start(), calls=%async_computation.33 | async-start | bytes 4866048
  591.9 342.5 %reduce-scatter.29.cloned.1.call-start = ((), (), s32[]{:S(2)}) async-start(), calls=%async_computation.34 | async-start | bytes 4866048
  597.0 479.1 %reduce-scatter.17.cloned.1.call-start = ((), (), s32[]{:S(2)}) async-start(), calls=%async_computation.18 | async-start | bytes 9732096 | tf_op jit(solution)/shard_map/reduce_scatter | solution.py:256
  603.2 614.4 %reduce-scatter.19.cloned.1.call-start = ((), (), s32[]{:S(2)}) async-start(), calls=%async_computation.19 | async-start | bytes 9732096 | tf_op jit(solution)/shard_map/reduce_scatter | solution.py:259
  608.3 644.9 %reduce-scatter.21.cloned.1.call-start = ((), (), s32[]{:S(2)}) async-start(), calls=%async_computation.21 | async-start | bytes 1966080 | tf_op jit(solution)/shard_map/reduce_scatter | solution.py:202
  626.3 663.4 %reduce-scatter.23.cloned.1.call-start = ((), (), s32[]{:S(2)}) async-start(), calls=%async_computation.23 | async-start | bytes 1966080 | tf_op jit(solution)/shard_map/reduce_scatter | solution.py:205
  673.9 652.2 %reduce-scatter.31.cloned.1.call-start = ((), (), s32[]{:S(2)}) async-start(), calls=%async_computation.35 | async-start | bytes 1966080
  712.9 671.6 %all-gather.42.cloned.1.call-start = ((), (), s32[]{:S(2)}) async-start(), calls=%async_computation.26 | async-start | bytes 2433024 | tf_op jit(solution)/shard_map/all_gather | solution.py:303
  823.7 619.5 %all-gather.44.cloned.1.call-start = ((), (), s32[]{:S(2)}) async-start(), calls=%async_computation.27 | async-start | bytes 2433024 | tf_op jit(solution)/shard_map/all_gather | solution.py:304
  936.1 573.5 %all-gather.40.cloned.1.call-start = ((), (), s32[]{:S(2)}) async-start(), calls=%async_computation.25 | async-start | bytes 4866048 | tf_op jit(solution)/shard_map/all_gather | solution.py:302
  1078.0 497.0 %all-gather.46.cloned.1.call-start = ((), (), s32[]{:S(2)}) async-start(), calls=%async_computation.28 | async-start | bytes 4866048 | tf_op jit(solution)/shard_map/all_gather | solution.py:305
  1219.5 452.4 %all-gather.48.cloned.1.call-start = ((), (), s32[]{:S(2)}) async-start(), calls=%async_computation.29 | async-start | bytes 12976128 | tf_op jit(solution)/shard_map/all_gather | solution.py:306
  1255.7 513.4 %all-gather.50.cloned.1.call-start = ((), (), s32[]{:S(2)}) async-start(), calls=%async_computation.30 | async-start | bytes 12976128 | tf_op jit(solution)/shard_map/all_gather | solution.py:307
  1292.2 596.2 %all-gather.52.cloned.1.call-start = ((), (), s32[]{:S(2)}) async-start(), calls=%async_computation.31 | async-start | bytes 12976128 | tf_op jit(solution)/shard_map/all_gather | solution.py:308
  2268.4 312.5 %all-to-all-start.2 = ((bf16[32,2,98304]{2,1,0:T(2,128)(2,1)}), bf16[32,2,98304]{2,1,0:T(2,128)(2,1)}, u32[]{:S(2)}, u32[]{:S(2)}) async-start(bf16[32,2,98304]{2,1,0:T(2,128)(2,1)} %reshape.307), calls=%async_computation.6 | async-start | bytes 25165824 | tf_op jit(solution)/shard_map/all_to_all | solution.py:347
  2275.0 164.1 %reduce-scatter.25.cloned.1.call-start = ((), (), s32[]{:S(2)}) async-start(), calls=%async_computation.32 | async-start | bytes 811008
  (43 other events, 4789.6 us)
Sparse Core Ops, SparseCore 0:
  10.9 56.3 all-gather.19
  70.2 55.7 all-gather.21
  129.0 63.0 all-gather.23
  194.9 61.9 all-gather.25
  259.5 93.2 all-gather.27
  355.6 93.7 all-gather.29
  452.2 93.7 all-gather.31
  558.1 53.0 all-gather.33
  613.2 54.2 all-gather.35
  669.2 38.6 all-gather.37
  713.9 108.0 reduce-scatter.26
  827.9 106.4 reduce-scatter.28
  940.9 135.1 reduce-scatter.16
  1082.5 135.0 reduce-scatter.18
  1255.4 34.2 reduce-scatter.22
  1291.8 34.2 reduce-scatter.30
  1328.9 55.4 all-gather.41
  1387.3 55.7 all-gather.43
  1446.5 63.0 all-gather.39
  1513.1 61.9 all-gather.45
  1578.5 93.2 all-gather.47
  1675.3 93.7 all-gather.49
  1772.3 116.0 all-gather.51
  2286.3 152.7 reduce-scatter.24
  (1 shorter events, 33.4 us)
where the time goes:
time: 2670 us; the launch traced here: 2660 us
  waiting for transfers between devices  1780 us (67%)
  matrix products  313 us (12%)
  local copies, waits for them, and re-layouts  238 us (9%)
  blocking collectives  196 us (7%)
  other arithmetic  109 us (4%)
    unnamed x29, waiting for transfers between devices  403 us
    reduce_scatter x1, waiting for transfers between devices, body(): lax.psum_scatter(grad_query, ('dp', 'fsdp'), scatter_dimension=0, tiled=T...  140 us
    reduce_scatter x1, waiting for transfers between devices, body(): lax.psum_scatter(grad_out, ('dp', 'fsdp'), scatter_dimension=0, tiled=True)  140 us
    all_gather x1, blocking collectives, body(): lax.all_gather(nesterov[0], ('dp', 'fsdp'), axis=1, tiled=True)  137 us
    unnamed x98, local copies, waits for them, and re-layouts  130 us
    all_gather x1, waiting for transfers between devices, body(): lax.all_gather(nesterov[7], ('dp', 'fsdp'), axis=0, tiled=True)  109 us
    all_gather x1, waiting for transfers between devices, body(): lax.all_gather(w_gate, ('dp', 'fsdp'), axis=0, tiled=True)  91.8 us
    all_gather x1, waiting for transfers between devices, body(): lax.all_gather(w_down, ('dp', 'fsdp'), axis=0, tiled=True)  88.8 us
  transfers between devices with their start and end apart: 26, of which 24 were waited for; matrix products, arithmetic and copies ran while one was open for 7% of the time, Pallas kernels for 0%

commit v1 on v0

v1 whole, which is shorter than its diff:
```python
import functools
import math

import jax
import jax.numpy as jnp
from jax import lax
from jax.experimental import pallas as pl
from jax.experimental.pallas import tpu as pltpu
from jax.sharding import PartitionSpec as P

D = 1536
HEADS = 16
KV_HEADS = 8
HEAD_DIM = 96
FF = 4096
KVW = 768

eps_norm = 1e-05
rope_base = 100000.0
coeff_a = 3.4445
coeff_b = -4.775
coeff_c = 2.0315
beta_moment = 0.95
rate_matrix = 0.2
rate_gain = 0.05
masked_score = -1e30

MESH = pl.DeviceIdType.MESH
low_type = jnp.bfloat16
wide_type = jnp.float32


class Place:
    def __init__(self, dp, fs):
        self.dp, self.fs, self.nd = dp, fs, dp * fs
        self.z = lax.axis_index("dp")
        self.f = lax.axis_index("fsdp")
        self.me = self.z * fs + self.f

    def of(self, index):
        return (index // self.fs, lax.rem(index, self.fs))


class Op:
    def __init__(self, source):
        self.source = source

    def scratch(self):
        return [
            pltpu.SemaphoreType.DMA,
            pltpu.SemaphoreType.DMA,
            pltpu.SemaphoreType.DMA,
            pltpu.VMEM(self.block_shape(), self.source.dtype),
        ]

    def block_shape(self):
        return self.source.shape[1:]

    def send(self, at, target):
        src, dst, (send_sem, recv_sem, _, _) = at
        return src, dst, send_sem, recv_sem

    def keep(self, at, src_block, dst_block):
        _, _, (_, _, own_sem, own) = at
        copy = pltpu.make_async_copy(src_block, own, own_sem)
        copy.start()
        copy.wait()
        copy = pltpu.make_async_copy(own, dst_block, own_sem)
        copy.start()
        copy.wait()

    def push(self, at, src_block, dst_block, device):
        _, _, (send_sem, recv_sem, _, _) = at
        pltpu.make_async_remote_copy(
            src_block, dst_block, send_sem, recv_sem, device_id=device, device_id_type=MESH
        ).start()

    def settle(self, at, sent, received):
        _, dst, (send_sem, recv_sem, _, _) = at
        if sent:
            part = dst.at[pl.ds(0, sent)]
            pltpu.make_async_copy(part, part, send_sem).wait()
        if received:
            part = dst.at[pl.ds(0, received)]
            pltpu.make_async_copy(part, part, recv_sem).wait()


class AllToAll(Op):
    def out(self, dp, fs):
        return jax.ShapeDtypeStruct((dp * fs,) + self.source.shape[1:], self.source.dtype)

    def pick(self, place, src, index):
        if self.source.shape[0] == place.nd:
            return src.at[index]
        return src.at[lax.rem(index, place.fs)]

    def start(self, place, at):
        src, dst, _ = at

        def step(k, carry):
            target = lax.rem(place.me + k, place.nd)
            self.push(at, self.pick(place, src, target), dst.at[place.me], place.of(target))
            return carry

        lax.fori_loop(1, place.nd, step, 0)
        self.keep(at, self.pick(place, src, place.me), dst.at[place.me])

    def finish(self, place, at):
        self.settle(at, place.nd - 1, place.nd - 1)


class SpreadAll(AllToAll):
    def block_shape(self):
        return self.source.shape

    def out(self, dp, fs):
        return jax.ShapeDtypeStruct((dp * fs,) + self.source.shape, self.source.dtype)

    def pick(self, place, src, index):
        return src


class PlaneAllToAll(Op):
    def out(self, dp, fs):
        return jax.ShapeDtypeStruct((fs,) + self.source.shape[1:], self.source.dtype)

    def pick(self, src, index):
        return src.at[index]

    def start(self, place, at):
        src, dst, _ = at

        def step(k, carry):
            target = lax.rem(place.f + k, place.fs)
            self.push(at, self.pick(src, target), dst.at[place.f], (place.z, target))
            return carry

        lax.fori_loop(1, place.fs, step, 0)
        self.keep(at, self.pick(src, place.f), dst.at[place.f])

    def finish(self, place, at):
        self.settle(at, place.fs - 1, place.fs - 1)


class PlaneSpread(PlaneAllToAll):
    def block_shape(self):
        return self.source.shape

    def out(self, dp, fs):
        return jax.ShapeDtypeStruct((fs,) + self.source.shape, self.source.dtype)

    def scratch(self):
        half = self.source_half
        return [
            pltpu.SemaphoreType.DMA,
            pltpu.SemaphoreType.DMA((half,)),
            pltpu.SemaphoreType.DMA,
            pltpu.VMEM(self.block_shape(), self.source.dtype),
            pltpu.SemaphoreType.DMA,
            pltpu.SemaphoreType.DMA,
        ]

    def __init__(self, source, fs):
        super().__init__(source)
        self.source_half = fs // 2

    def start(self, place, at):
        src, dst, (send_sem, recv_sems, own_sem, own, pair_send, pair_recv) = at
        core = lax.rem(place.f, 2)
        chip = place.f // 2
        half = place.fs // 2
        for k in range(1, half):
            target = lax.rem(chip + k, half)
            pltpu.make_async_remote_copy(
                src,
                dst.at[place.f],
                send_sem,
                recv_sems.at[k],
                device_id=(place.z, 2 * target + core),
                device_id_type=MESH,
            ).start()
        pltpu.make_async_remote_copy(
            src,
            dst.at[place.f],
            pair_send,
            pair_recv,
            device_id=(place.z, 2 * chip + 1 - core),
            device_id_type=MESH,
        ).start()
        copy = pltpu.make_async_copy(src, own, own_sem)
        copy.start()
        copy.wait()
        copy = pltpu.make_async_copy(own, dst.at[place.f], own_sem)
        copy.start()
        copy.wait()

    def finish(self, place, at):
        src, dst, (send_sem, recv_sems, own_sem, own, pair_send, pair_recv) = at
        core = lax.rem(place.f, 2)
        chip = place.f // 2
        half = place.fs // 2
        for k in range(1, half):
            origin = 2 * lax.rem(chip + half - k, half) + core
            block = dst.at[origin]
            pltpu.make_async_copy(block, block, recv_sems.at[k]).wait()
            pltpu.make_async_remote_copy(
                block,
                block,
                pair_send,
                pair_recv,
                device_id=(place.z, 2 * chip + 1 - core),
                device_id_type=MESH,
            ).start()
        if half > 1:
            part = dst.at[pl.ds(0, half - 1)]
            pltpu.make_async_copy(part, part, send_sem).wait()
        part = dst.at[pl.ds(0, half)]
        pltpu.make_async_copy(part, part, pair_send).wait()
        pltpu.make_async_copy(part, part, pair_recv).wait()


class ChainAllToAll(Op):
    def out(self, dp, fs):
        return jax.ShapeDtypeStruct((dp,) + self.source.shape[1:], self.source.dtype)

    def pick(self, src, index):
        return src.at[index]

    def start(self, place, at):
        src, dst, _ = at

        def step(k, carry):
            target = lax.rem(place.z + k, place.dp)
            self.push(at, self.pick(src, target), dst.at[place.z], (target, place.f))
            return carry

        lax.fori_loop(1, place.dp, step, 0)
        self.keep(at, self.pick(src, place.z), dst.at[place.z])

    def finish(self, place, at):
        self.settle(at, place.dp - 1, place.dp - 1)


class ChainSpread(ChainAllToAll):
    def block_shape(self):
        return self.source.shape

    def out(self, dp, fs):
        return jax.ShapeDtypeStruct((dp,) + self.source.shape, self.source.dtype)

    def pick(self, src, index):
        return src


class OutRows(Op):
    def block_shape(self):
        return self.source.shape

    def out(self, dp, fs):
        return jax.ShapeDtypeStruct((dp,) + self.source.shape, self.source.dtype)

    def start(self, place, at):
        src, dst, _ = at
        column, slot = place.me // place.dp, lax.rem(place.me, place.dp)
        for q in range(place.dp):
            own = (place.z == q) & (place.f == column)

            @pl.when(own)
            def _():
                self.keep(at, src, dst.at[slot])

            @pl.when(jnp.logical_not(own))
            def _():
                self.push(at, src, dst.at[slot], (q, column))

    def finish(self, place, at):
        mine = place.me // place.dp == place.f

        @pl.when(mine)
        def _():
            self.settle(at, place.dp - 1, place.dp - 1)

        @pl.when(jnp.logical_not(mine))
        def _():
            self.settle(at, place.dp, place.dp)


class OutGrads(Op):
    def out(self, dp, fs):
        return jax.ShapeDtypeStruct((dp,) + self.source.shape[1:], self.source.dtype)

    def start(self, place, at):
        src, dst, _ = at
        for i in range(place.dp):
            owner = place.f * place.dp + i

            @pl.when(owner == place.me)
            def _():
                self.keep(at, src.at[i], dst.at[place.z])

            @pl.when(owner != place.me)
            def _():
                self.push(at, src.at[i], dst.at[place.z], place.of(owner))

    def finish(self, place, at):
        mine = place.me // place.dp == place.f

        @pl.when(mine)
        def _():
            self.settle(at, place.dp - 1, place.dp - 1)

        @pl.when(jnp.logical_not(mine))
        def _():
            self.settle(at, place.dp, place.dp)


class ToOwners(Op):
    def __init__(self, source, owner_ids):
        super().__init__(source)
        self.owner_ids = owner_ids

    def out(self, dp, fs):
        return jax.ShapeDtypeStruct((dp * fs,) + self.source.shape[1:], self.source.dtype)

    def start(self, place, at):
        src, dst, _ = at
        for i, owner in enumerate(self.owner_ids):

            @pl.when(place.me != owner)
            def _():
                self.push(at, src.at[i], dst.at[place.me], (owner // place.fs, owner % place.fs))

        for i, owner in enumerate(self.owner_ids):

            @pl.when(place.me == owner)
            def _():
                self.keep(at, src.at[i], dst.at[place.me])

    def finish(self, place, at):
        count = len(self.owner_ids)
        owns = functools.reduce(lambda x, y: x | y, [place.me == o for o in self.owner_ids])

        @pl.when(owns)
        def _():
            self.settle(at, count - 1, place.nd - 1)

        @pl.when(jnp.logical_not(owns))
        def _():
            self.settle(at, count, 0)


class FromOwners(Op):
    def __init__(self, source, owner_ids):
        super().__init__(source)
        self.owner_ids = owner_ids

    def out(self, dp, fs):
        return jax.ShapeDtypeStruct((len(self.owner_ids),) + self.source.shape[1:], self.source.dtype)

    def start(self, place, at):
        src, dst, _ = at
        for i, owner in enumerate(self.owner_ids):

            @pl.when(place.me == owner)
            def _():
                def step(k, carry):
                    target = lax.rem(place.me + k, place.nd)
                    self.push(at, src.at[target], dst.at[i], place.of(target))
                    return carry

                lax.fori_loop(1, place.nd, step, 0)
                self.keep(at, src.at[place.me], dst.at[i])

    def finish(self, place, at):
        _, dst, (send_sem, recv_sem, _, _) = at
        src = at[0]
        count = len(self.owner_ids)
        owns = functools.reduce(lambda x, y: x | y, [place.me == o for o in self.owner_ids])

        @pl.when(owns)
        def _():
            part = src.at[pl.ds(0, place.nd - 1)]
            pltpu.make_async_copy(part, part, send_sem).wait()
            if count > 1:
                part = dst.at[pl.ds(0, count - 1)]
                pltpu.make_async_copy(part, part, recv_sem).wait()

        @pl.when(jnp.logical_not(owns))
        def _():
            part = dst.at[pl.ds(0, count)]
            pltpu.make_async_copy(part, part, recv_sem).wait()


def move(number, dp, fs, *ops):
    count = len(ops)
    scratch = [op.scratch() for op in ops]
    lengths = [len(part) for part in scratch]

    def kernel(*refs):
        place = Place(dp, fs)
        sources, targets, rest = refs[:count], refs[count : 2 * count], list(refs[2 * count :])
        parts = []
        for i in range(count):
            parts.append((sources[i], targets[i], tuple(rest[: lengths[i]])))
            rest = rest[lengths[i] :]
        barrier = pltpu.get_barrier_semaphore()

        def greet(k, carry):
            pl.semaphore_signal(
                barrier, inc=1, device_id=place.of(lax.rem(place.me + k, place.nd)), device_id_type=MESH
            )
            return carry

        lax.fori_loop(1, place.nd, greet, 0)
        pl.semaphore_wait(barrier, place.nd - 1)
        for op, at in zip(ops, parts):
            op.start(place, at)
        for op, at in zip(ops, parts):
            op.finish(place, at)

    return pl.pallas_call(
        kernel,
        out_shape=tuple(op.out(dp, fs) for op in ops),
        in_specs=[pl.BlockSpec(memory_space=pl.ANY)] * count,
        out_specs=tuple([pl.BlockSpec(memory_space=pl.ANY)] * count),
        scratch_shapes=sum(scratch, []),
        compiler_params=pltpu.CompilerParams(collective_id=number, has_side_effects=True),
        name=f"move_{number}",
    )(*[op.source for op in ops])


def rope_tables(length, head_width):
    half_width = head_width // 2
    frequency = rope_base ** (-(jnp.arange(half_width, dtype=jnp.float32) * 2.0 / head_width))
    angles = jnp.arange(length, dtype=jnp.float32)[:, None] * frequency[None, :]
    return (jnp.cos(angles)[:, None, :], jnp.sin(angles)[:, None, :])


def rotate(head_rows, cosine, sine_table):
    half_width = head_rows.shape[-1] // 2
    leading = head_rows[..., :half_width]
    trailing = head_rows[..., half_width:]
    return jnp.concatenate(
        [leading * cosine - trailing * sine_table, trailing * cosine + leading * sine_table],
        axis=-1,
    )


def unrotate(grad_rows, cosine, sine_table):
    half_width = grad_rows.shape[-1] // 2
    leading = grad_rows[..., :half_width]
    trailing = grad_rows[..., half_width:]
    return jnp.concatenate(
        [leading * cosine + trailing * sine_table, trailing * cosine - leading * sine_table],
        axis=-1,
    )


def rms_inverse(activation):
    return lax.rsqrt(jnp.mean(activation * activation, axis=-1, keepdims=True) + eps_norm)


def rms_back(grad_normed, normed, inverse):
    return inverse * (grad_normed - normed * jnp.mean(grad_normed * normed, axis=-1, keepdims=True))


def mul(left_side, right_side):
    return jnp.dot(left_side, right_side, preferred_element_type=wide_type)


def mul_bt(left_side, right_side):
    return jnp.einsum("ik,jk->ij", left_side, right_side, preferred_element_type=wide_type)


def mul_at(left_side, right_side):
    return jnp.einsum("ki,kj->ij", left_side, right_side, preferred_element_type=wide_type)


def gram_mixer(gram):
    a = coeff_a
    frobenius = jnp.sqrt(jnp.trace(gram))
    scale = 1.0 / (frobenius + 1e-07)
    gram_low = (gram * (scale * scale)).astype(low_type)
    parts = []
    for number in range(3):
        square = mul(gram_low, gram_low)
        part = (coeff_b * gram_low.astype(wide_type) + coeff_c * square).astype(low_type)
        parts.append(part)
        if number < 2:
            half = mul(part, gram_low).astype(low_type)
            gram_low = (
                a * a * gram_low.astype(wide_type)
                + 2.0 * a * half.astype(wide_type)
                + mul(part, half)
            ).astype(low_type)
    first, second, third = parts
    joint = (
        a * (first.astype(wide_type) + second.astype(wide_type)) + mul(second, first)
    ).astype(low_type)
    mixer = a * a * third.astype(wide_type) + a * joint.astype(wide_type) + mul(third, joint)
    return scale, mixer.astype(low_type)


def body(
    tokens,
    segments,
    cotangent,
    norm_gains,
    w_query,
    w_key,
    w_value,
    w_out,
    w_gate,
    w_up,
    w_down,
    moment_gains,
    moment_query,
    moment_key,
    moment_value,
    moment_out,
    moment_gate,
    moment_up,
    moment_down,
):
    dp, fs = lax.axis_size("dp"), lax.axis_size("fsdp")
    nd = dp * fs
    me = lax.axis_index("dp") * fs + lax.axis_index("fsdp")
    place_f = lax.axis_index("fsdp")
    length = tokens.shape[0]
    rows = D // nd
    ff_rows = FF // nd
    ff_part = FF // fs
    q_heads = HEADS // fs
    kv_heads = max(1, KV_HEADS // fs)
    repeat = max(1, fs // KV_HEADS)
    group = q_heads // kv_heads
    q_width, kv_width = q_heads * HEAD_DIM, kv_heads * HEAD_DIM
    go = functools.partial(move, dp=dp, fs=fs)

    def run(number, *ops):
        return move(number, dp, fs, *ops)

    def kv_blocks(weight):
        blocks = weight.reshape(rows, KV_HEADS // kv_heads, kv_width)
        return jnp.repeat(blocks, repeat, axis=1) if repeat > 1 else blocks

    def ff_blocks(weight):
        return (
            weight.reshape(rows, dp, fs, ff_rows).transpose(2, 0, 1, 3).reshape(fs, rows, ff_part)
        )

    qkv_blocks = jnp.concatenate(
        [w_query.reshape(rows, fs, q_width), kv_blocks(w_key), kv_blocks(w_value)], axis=-1
    ).transpose(1, 0, 2)
    qkv_width = q_width + 2 * kv_width

    token_all, segment_all, qkv_all, out_all, gain_all = run(
        0,
        PlaneSpread(tokens, fs),
        PlaneAllToAll(jnp.broadcast_to(segments[None], (fs,) + segments.shape)),
        AllToAll(qkv_blocks),
        OutRows(w_out),
        SpreadAll(norm_gains),
    )
    gain_rows = gain_all.transpose(1, 0, 2).reshape(2, D).astype(wide_type)
    qkv_weight = qkv_all.reshape(D, qkv_width)
    out_weight = out_all.reshape(D // fs, D)

    count = fs * length
    cosine, sine_table = rope_tables(length, HEAD_DIM)
    score_scale = 1.0 / math.sqrt(HEAD_DIM)
    plane_in = token_all.reshape(count, D).astype(wide_type)
    entry_one = (plane_in * rms_inverse(plane_in) * gain_rows[0]).astype(low_type)
    qkv_pre = mul(entry_one, qkv_weight)
    query_rot = rotate(
        qkv_pre[:, :q_width].reshape(fs, length, q_heads, HEAD_DIM), cosine, sine_table
    ).astype(low_type)
    key_rot = rotate(
        qkv_pre[:, q_width : q_width + kv_width].reshape(fs, length, kv_heads, HEAD_DIM),
        cosine,
        sine_table,
    ).astype(low_type)
    values = (
        qkv_pre[:, q_width + kv_width :].reshape(fs, length, kv_heads, HEAD_DIM).astype(low_type)
    )
    query_rot = query_rot.reshape(fs, length, kv_heads, group, HEAD_DIM)
    segment_rows = segment_all.reshape(fs, length)
    positions = jnp.arange(length)
    allowed = (segment_rows[:, :, None] == segment_rows[:, None, :]) & (
        positions[None, None, :] <= positions[None, :, None]
    )
    raw_scores = jnp.einsum(
        "sqhgd,skhd->shgqk", query_rot, key_rot, preferred_element_type=wide_type
    )
    scores = jnp.where(allowed[:, None, None], raw_scores * score_scale, masked_score)
    row_max = jnp.max(scores, axis=-1, keepdims=True)
    expo_rows = jnp.exp(scores - row_max)
    attention = expo_rows / jnp.sum(expo_rows, axis=-1, keepdims=True)
    attention_low = attention.astype(low_type)
    attn_low = (
        jnp.einsum("shgqk,skhd->sqhgd", attention_low, values, preferred_element_type=wide_type)
        .reshape(count, q_width)
        .astype(low_type)
    )
    hidden_part = mul(attn_low, out_weight).astype(low_type).reshape(fs, length, D)

    hidden_all, gate_all = run(1, PlaneAllToAll(hidden_part), AllToAll(ff_blocks(w_gate)))
    residual_in = tokens.astype(wide_type)
    hidden = residual_in + jnp.sum(hidden_all.astype(wide_type), axis=0)
    inverse_two = rms_inverse(hidden)
    normed_two = hidden * inverse_two
    entry_two = (normed_two * gain_rows[1]).astype(low_type)

    entry_all, up_all = run(2, PlaneSpread(entry_two, fs), AllToAll(ff_blocks(w_up)))
    entry_all = entry_all.reshape(count, D)
    gate_weight = gate_all.reshape(D, ff_part)
    up_weight = up_all.reshape(D, ff_part)
    gate_pre = mul(entry_all, gate_weight)
    up_pre = mul(entry_all, up_weight)
    gate_sig = jax.nn.sigmoid(gate_pre)
    act_low = (gate_pre * gate_sig * up_pre).astype(low_type)

    cot_all, down_all = run(3, PlaneSpread(cotangent, fs), ChainSpread(w_down))
    cot_all = cot_all.reshape(count, D)
    down_weight = down_all.reshape(ff_part, D)
    down_part = mul(act_low, down_weight).astype(low_type).reshape(fs, length, D)
    d_act = mul_bt(cot_all, down_weight)
    d_gate_low = (d_act * up_pre * gate_sig * (1.0 + gate_pre * (1.0 - gate_sig))).astype(low_type)
    d_up_low = (d_act * gate_pre * gate_sig).astype(low_type)
    d_entry_part = (mul_bt(d_gate_low, gate_weight) + mul_bt(d_up_low, up_weight)).astype(low_type)
    grad_down_part = mul_at(act_low, cot_all).astype(low_type).reshape(dp, ff_rows, D)
    grad_gate_part = mul_at(entry_all, d_gate_low).astype(low_type).reshape(nd, rows, ff_part)
    grad_up_part = mul_at(entry_all, d_up_low).astype(low_type).reshape(nd, rows, ff_part)

    down_out, d_entry_all, grad_down_all = run(
        4,
        PlaneAllToAll(down_part),
        PlaneAllToAll(d_entry_part.reshape(fs, length, D)),
        ChainAllToAll(grad_down_part),
    )
    outputs = (hidden + jnp.sum(down_out.astype(wide_type), axis=0)).astype(low_type)
    d_entry_two = jnp.sum(d_entry_all.astype(wide_type), axis=0)
    grad_down = jnp.sum(grad_down_all.astype(wide_type), axis=0)
    cot_float = cotangent.astype(wide_type)
    d_hidden = cot_float + rms_back(d_entry_two * gain_rows[1], normed_two, inverse_two)
    d_hidden_low = d_hidden.astype(low_type)

    d_hidden_all, grad_gate_all = run(
        5, PlaneSpread(d_hidden_low, fs), AllToAll(grad_gate_part)
    )
    d_hidden_all = d_hidden_all.reshape(count, D)
    d_attn = mul_bt(d_hidden_all, out_weight).astype(low_type)
    grad_out_part = mul_at(attn_low, d_hidden_all).astype(low_type).reshape(dp, rows, D)
    d_attn = d_attn.reshape(fs, length, kv_heads, group, HEAD_DIM)
    d_probs = jnp.einsum("sqhgd,skhd->shgqk", d_attn, values, preferred_element_type=wide_type)
    d_values = jnp.einsum(
        "shgqk,sqhgd->skhd", attention_low, d_attn, preferred_element_type=wide_type
    )
    row_delta = jnp.sum(attention * d_probs, axis=-1, keepdims=True)
    d_scores = (attention * (d_probs - row_delta)).astype(low_type)
    d_query_rot = (
        jnp.einsum("shgqk,skhd->sqhgd", d_scores, key_rot, preferred_element_type=wide_type)
        * score_scale
    )
    d_key_rot = (
        jnp.einsum("shgqk,sqhgd->skhd", d_scores, query_rot, preferred_element_type=wide_type)
        * score_scale
    )
    d_query = unrotate(d_query_rot.reshape(fs, length, q_heads, HEAD_DIM), cosine, sine_table)
    d_key = unrotate(d_key_rot, cosine, sine_table)
    d_qkv = jnp.concatenate(
        [
            d_query.reshape(count, q_width),
            d_key.reshape(count, kv_width),
            d_values.reshape(count, kv_width),
        ],
        axis=-1,
    ).astype(low_type)
    grad_qkv_part = mul_at(entry_one, d_qkv).astype(low_type).reshape(nd, rows, qkv_width)
    d_first_part = mul_bt(d_qkv, qkv_weight).astype(low_type).reshape(fs, length, D)

    d_first_all, grad_up_all = run(6, PlaneAllToAll(d_first_part), AllToAll(grad_up_part))
    d_entry_one = jnp.sum(d_first_all.astype(wide_type), axis=0)
    inverse_one = rms_inverse(residual_in)
    normed_one = residual_in * inverse_one
    grad_tokens = d_hidden + rms_back(d_entry_one * gain_rows[0], normed_one, inverse_one)
    grad_gain_part = (
        jnp.stack([jnp.sum(d_entry_one * normed_one, axis=0), jnp.sum(d_entry_two * normed_two, axis=0)])
        .reshape(2, nd, rows)
        .transpose(1, 0, 2)
    )

    grad_qkv_all, grad_out_all, grad_gain_all = run(
        7, AllToAll(grad_qkv_part), OutGrads(grad_out_part), AllToAll(grad_gain_part)
    )

    def ff_rows_of(blocks):
        total = jnp.sum(blocks.reshape(dp, fs, rows, ff_part).astype(wide_type), axis=0)
        return total.reshape(fs, rows, dp, ff_rows).transpose(1, 2, 0, 3).reshape(rows, FF)

    qkv_total = jnp.sum(grad_qkv_all.reshape(dp, fs, rows, qkv_width).astype(wide_type), axis=0)
    grad_query = qkv_total[..., :q_width].transpose(1, 0, 2).reshape(rows, D)

    def kv_rows_of(blocks):
        if repeat > 1:
            blocks = jnp.sum(blocks.reshape(fs // repeat, repeat, rows, kv_width), axis=1)
        return blocks.transpose(1, 0, 2).reshape(rows, KVW)

    grad_key = kv_rows_of(qkv_total[..., q_width : q_width + kv_width])
    grad_value = kv_rows_of(qkv_total[..., q_width + kv_width :])
    summed = (
        jnp.sum(grad_gain_all, axis=0),
        grad_query,
        grad_key,
        grad_value,
        jnp.sum(grad_out_all.astype(wide_type), axis=0),
        ff_rows_of(grad_gate_all),
        ff_rows_of(grad_up_all),
        grad_down,
    )
    moments_old = (
        moment_gains,
        moment_query,
        moment_key,
        moment_value,
        moment_out,
        moment_gate,
        moment_up,
        moment_down,
    )
    new_moments = tuple(beta_moment * old + grad for old, grad in zip(moments_old, summed))
    nesterov = tuple(
        (grad + beta_moment * now).astype(low_type) for grad, now in zip(summed, new_moments)
    )

    def linear(z_at, f_at):
        return (z_at % dp) * fs + f_at % fs

    gate_owner, up_owner = linear(1, 0), linear(1, fs - 2)
    down_owner = linear(2, 2)
    query_owner, out_owner = linear(2, 4), linear(0, fs - 2)
    key_owner, value_owner = linear(3, 0), linear(3, 4)
    gain_whole, wide_all, tall_all, square_all, small_all = run(
        8,
        SpreadAll(nesterov[0]),
        ToOwners(jnp.stack([nesterov[5], nesterov[6]]), (gate_owner, up_owner)),
        ToOwners(nesterov[7][None], (down_owner,)),
        ToOwners(jnp.stack([nesterov[1], nesterov[4]]), (query_owner, out_owner)),
        ToOwners(jnp.stack([nesterov[2], nesterov[3]]), (key_owner, value_owner)),
    )
    role = jnp.where(
        (me == gate_owner) | (me == up_owner),
        1,
        jnp.where(
            me == down_owner,
            2,
            jnp.where(
                (me == query_owner) | (me == out_owner),
                3,
                jnp.where((me == key_owner) | (me == value_owner), 4, 0),
            ),
        ),
    )

    def idle_work(wide, tall, square, small):
        return wide, tall, square, small

    def step_rows(block, scale, mixer):
        return (
            coeff_a**3 * scale * block.astype(wide_type) + scale * mul(block, mixer)
        ).astype(low_type)

    def wide_work(wide, tall, square, small):
        matrix = wide.reshape(D, FF)
        scale, mixer = gram_mixer(mul_bt(matrix, matrix))
        result = coeff_a**3 * scale * matrix.astype(wide_type) + scale * mul(mixer, matrix)
        return result.astype(low_type).reshape(wide.shape), tall, square, small

    def rows_work(slot, width):
        def work(*blocks):
            blocks = list(blocks)
            matrix = blocks[slot].reshape(-1, width)
            scale, mixer = gram_mixer(mul_at(matrix, matrix))
            blocks[slot] = step_rows(matrix, scale, mixer).reshape(blocks[slot].shape)
            return tuple(blocks)

        return work

    wide_all, tall_all, square_all, small_all = lax.switch(
        role,
        [idle_work, wide_work, rows_work(1, D), rows_work(2, D), rows_work(3, KVW)],
        wide_all,
        tall_all,
        square_all,
        small_all,
    )
    wide_new, tall_new, square_new, small_new = run(
        9,
        FromOwners(wide_all, (gate_owner, up_owner)),
        FromOwners(tall_all, (down_owner,)),
        FromOwners(square_all, (query_owner, out_owner)),
        FromOwners(small_all, (key_owner, value_owner)),
    )
    gain_dir = gain_whole.transpose(1, 0, 2).reshape(2, D).astype(wide_type)
    gain_scale = lax.rsqrt(jnp.mean(gain_dir * gain_dir, axis=-1, keepdims=True) + 1e-06)
    updates = [-rate_gain * nesterov[0].astype(wide_type) * gain_scale]
    pieces = (
        (square_new[0], D, D),
        (small_new[0], D, KVW),
        (small_new[1], D, KVW),
        (square_new[1], D, D),
        (wide_new[0], D, FF),
        (wide_new[1], D, FF),
        (tall_new[0], FF, D),
    )
    for piece, row_count, col_count in pieces:
        factor = math.sqrt(max(1.0, col_count / row_count))
        updates.append(-rate_matrix * factor * piece.astype(wide_type))
    return (outputs, grad_tokens) + summed + tuple(updates) + new_moments


def solution(mesh):
    by_rows = P(("dp", "fsdp"), None)
    by_columns = P(None, ("dp", "fsdp"))
    per_parameter = (by_columns,) + (by_rows,) * 7
    return jax.shard_map(
        body,
        mesh=mesh,
        in_specs=(by_rows,) * 3 + per_parameter * 2,
        out_specs=(by_rows,) * 2 + per_parameter * 3,
        check_vma=False,
    )
```

time: 2670 us -> 945 us (0.35)
  waiting for transfers between devices: 1780 us -> 0 us
  Pallas kernels: 0 us -> 647 us
  local copies, waits for them, and re-layouts: 238 us -> 29.2 us
  blocking collectives: 196 us -> 0 us
  matrix products: 313 us -> 185 us
  other arithmetic: 109 us -> 61.7 us
    all_gather x17 -> x0, waiting for transfers between devices: 1030 us -> none  [the longest x1 109 us: body(): lax.all_gather(nesterov[7], ('dp', 'fsdp'), axis=0, tiled=True)]
    pallas_call x0 -> x10, Pallas kernels: none -> 647 us  [move(): pl.pallas_call(kernel, out_shape=tuple((op.out(dp, fs) for op in ops)), i...]
    unnamed x29 -> x0, waiting for transfers between devices: 403 us -> none
    reduce_scatter x4 -> x0, waiting for transfers between devices: 347 us -> none  [the longest x1 140 us: body(): lax.psum_scatter(grad_query, ('dp', 'fsdp'), scatter_dimension=0, tiled=T...]
    all_gather x2 -> x0, blocking collectives: 166 us -> none  [the longest x1 137 us: body(): lax.all_gather(nesterov[0], ('dp', 'fsdp'), axis=1, tiled=True)]
    unnamed x98 -> x119, local copies, waits for them, and re-layouts: 130 us -> 5.39 us
    dot_general x34 -> x32, matrix products: 306 us -> 185 us  [the longest x15 123 us: mul(): return jnp.dot(left_side, right_side, preferred_element_type=wide_type)]
    reshape x9 -> x15, local copies, waits for them, and re-layouts: 56.6 us -> 10 us  [the longest x2 3.66 us: ff_rows_of(): total.reshape(fs, rows, dp, ff_rows).transpose(1, 2, 0, 3).reshape(rows, FF)]
  transfers between devices with their start and end apart: 26 -> 0, of which waited for: 24 -> 0; matrix products, arithmetic and copies ran while one was open for 7% -> 0% of each run, Pallas kernels for 0% -> 0%
where the time goes in v1:
time: 945 us; the launch traced here: 934 us
  Pallas kernels  647 us (68%)
  matrix products  185 us (20%)
  other arithmetic  61.7 us (7%)
  local copies, waits for them, and re-layouts  29.2 us (3%)
    pallas_call x10, Pallas kernels, move(): pl.pallas_call(kernel, out_shape=tuple((op.out(dp, fs) for op in ops)), i...  647 us
    dot_general x15, matrix products, mul(): return jnp.dot(left_side, right_side, preferred_element_type=wide_type)  123 us
    dot_general x6, matrix products, mul_bt(): jnp.einsum('ik,jk->ij', left_side, right_side, preferred_element_type=wid...  42.9 us

profile of v1, /device:TPU:14, one launch (start us, length us, event | category | flops | bytes accessed | tf_op | source)
XLA Modules:
  0.0 934.0 jit_solution(2196543492759405395)
XLA Ops:
  9.6 53.2 %move_0.1 = (bf16[8,128,1536]{2,1,0:T(8,128)(2,1)}, s32[8,1,128]{2,1,0:T(1,128)}, bf16[32,48,384]{2,1,0:T(8,128)(2,1)}, bf16[4,48,1536]{2,1,0:T(8,128)(2,1)}, bf16[32,2,48]{2,1,0:T(2,128)(2,1)}) custom-call(bf16[128,1536]{1,0:T(8,128)(2,1)} %refs_0_.2, s32[8,1,128]{2,1,0:T(1,128)} %broadcast_in_dim.52.refs_1_, ...), custom_call_target="tpu_custom_call" | custom-call | tf_op jit(solution)/shard_map/move_0/pallas_call | solution.py:421
  79.1 56.9 %move_1.1 = (bf16[8,128,1536]{2,1,0:T(8,128)(2,1)}, bf16[32,48,512]{2,1,0:T(8,128)(2,1)}) custom-call(bf16[8,128,1536]{2,1,0:T(8,128)(2,1)} %bitcast.398, bf16[8,48,512]{2,1,0:T(8,128)(2,1)} %reshape.450.refs_1_), custom_call_target="tpu_custom_call" | custom-call | tf_op jit(solution)/shard_map/move_1/pallas_call | solution.py:421
  140.0 45.7 %move_2.1 = (bf16[8,128,1536]{2,1,0:T(8,128)(2,1)}, bf16[32,48,512]{2,1,0:T(8,128)(2,1)}) custom-call(bf16[128,1536]{1,0:T(8,128)(2,1)} %multiply_convert_fusion.6.refs_0_, bf16[8,48,512]{2,1,0:T(8,128)(2,1)} %reshape.452.refs_1_), custom_call_target="tpu_custom_call" | custom-call | tf_op jit(solution)/shard_map/move_2/pallas_call | solution.py:421
  185.7 5.7 fusion.114
  194.5 41.9 %move_3.1 = (bf16[8,128,1536]{2,1,0:T(8,128)(2,1)}, bf16[4,128,1536]{2,1,0:T(8,128)(2,1)}) custom-call(bf16[128,1536]{1,0:T(8,128)(2,1)} %refs_0_.3, bf16[128,1536]{1,0:T(8,128)(2,1)} %refs_1_.1), custom_call_target="tpu_custom_call" | custom-call | tf_op jit(solution)/shard_map/move_3/pallas_call | solution.py:421
  236.4 6.4 multiply_convert_fusion.2
  260.7 70.8 %move_4.1 = (bf16[8,128,1536]{2,1,0:T(8,128)(2,1)}, bf16[8,128,1536]{2,1,0:T(8,128)(2,1)}, bf16[4,128,1536]{2,1,0:T(8,128)(2,1)}) custom-call(bf16[8,128,1536]{2,1,0:T(8,128)(2,1)} %bitcast.414, bf16[8,128,1536]{2,1,0:T(8,128)(2,1)} %bitcast.403, bf16[4,128,1536]{2,1,0:T(8,128)(2,1)} %bitcast.429), custom_call_target="tpu_custom_call" | custom-call | tf_op jit(solution)/shard_map/move_4/pallas_call | solution.py:421
  341.2 45.7 %move_5.1 = (bf16[8,128,1536]{2,1,0:T(8,128)(2,1)}, bf16[32,48,512]{2,1,0:T(8,128)(2,1)}) custom-call(bf16[128,1536]{1,0:T(8,128)(2,1)} %fusion.106.refs_0_, bf16[32,48,512]{2,1,0:T(8,128)(2,1)} %bitcast.426), custom_call_target="tpu_custom_call" | custom-call | tf_op jit(solution)/shard_map/move_5/pallas_call | solution.py:421
  408.8 56.2 %move_6.1 = (bf16[8,128,1536]{2,1,0:T(8,128)(2,1)}, bf16[32,48,512]{2,1,0:T(8,128)(2,1)}) custom-call(bf16[8,128,1536]{2,1,0:T(8,128)(2,1)} %bitcast.408, bf16[32,48,512]{2,1,0:T(8,128)(2,1)} %bitcast.425), custom_call_target="tpu_custom_call" | custom-call | tf_op jit(solution)/shard_map/move_6/pallas_call | solution.py:421
  477.1 63.5 %move_7.1 = (bf16[32,48,384]{2,1,0:T(8,128)(2,1)}, bf16[4,48,1536]{2,1,0:T(8,128)(2,1)}, f32[32,2,48]{2,1,0:T(2,128)}) custom-call(bf16[32,48,384]{2,1,0:T(8,128)(2,1)} %bitcast.430, bf16[4,48,1536]{2,1,0:T(8,128)(2,1)} %bitcast.416, f32[32,2,48]{2,1,0:T(2,128)} %maximum_bitcast_fusion.4.refs_2_), custom_call_target="tpu_custom_call" | custom-call | tf_op jit(solution)/shard_map/move_7/pallas_call | solution.py:421
  560.7 76.7 %move_8.1 = (bf16[32,2,48]{2,1,0:T(2,128)(2,1)}, bf16[32,48,4096]{2,1,0:T(8,128)(2,1)}, bf16[32,128,1536]{2,1,0:T(8,128)(2,1)}, bf16[32,48,1536]{2,1,0:T(8,128)(2,1)}, bf16[32,48,768]{2,1,0:T(8,128)(2,1)}) custom-call(bf16[2,48]{1,0:T(2,128)(2,1)} %get-tuple-element.237.refs_0_, bf16[2,48,4096]{2,1,0:T(8,128)(2,1)} %pad_maximum_fusion.refs_1_, ...), custom_call_target="tpu_custom_call" | custom-call | tf_op jit(solution)/shard_map/move_8/pallas_call | solution.py:421
  639.0 150.0 %conditional.1 = (bf16[32,48,4096]{2,1,0:T(8,128)(2,1)}, bf16[32,48,1536]{2,1,0:T(8,128)(2,1)}, bf16[32,48,768]{2,1,0:T(8,128)(2,1)}, bf16[32,128,1536]{2,1,0:T(8,128)(2,1)}) conditional(s32[]{:T(128)} %clamp.3, (bf16[32,48,4096]{2,1,0:T(8,128)(2,1)}, bf16[32,128,1536]{2,1,0:T(8,128)(2,1)}, ...), branch_computations={%region_21.22_spmd, %region_22.24_spmd, %region_24.26_spmd, %regio... | conditional | flops 104031584256 | bytes 320864512 | solution.py:789
  643.5 24.4 %select_reduce_fusion = (f32[]{:T(128)}, f32[1536,1536]{1,0:T(8,128)}) fusion(bf16[1536,4096]{1,0:T(8,128)(2,1)S(1)} %copy.247), kind=kOutput, calls=%fused_computation.22 | convolution fusion | flops 19334430720 | bytes 22020100 | tf_op jit(solution)/shard_map/cond/branch_1_fun/ik,jk->ij/dot_general | solution.py:472
  673.6 8.5 fusion.4
  682.0 7.8 convolution_convert_fusion.1
  689.8 8.7 fusion.2
  698.5 8.6 fusion.9
  707.1 10.0 %add_convert_fusion.2 = bf16[1536,1536]{1,0:T(8,128)(2,1)} fusion(bf16[1536,1536]{1,0:T(8,128)(2,1)S(1)} %fusion.9, bf16[1536,1536]{1,0:T(8,128)(2,1)S(1)} %fusion.4), kind=kOutput, calls=%fused_computation.19 | convolution fusion | flops 7261913088 | bytes 14155776 | tf_op jit(solution)/shard_map/cond/branch_1_fun/dot_general | solution.py:468
  717.1 7.7 convolution_convert_fusion
  724.8 10.2 %fusion.7 = bf16[1536,1536]{1,0:T(8,128)(2,1)} fusion(bf16[1536,1536]{1,0:T(8,128)(2,1)S(1)} %fusion.2, bf16[1536,1536]{1,0:T(8,128)(2,1)S(1)} %convolution_convert_fusion, bf16[1536,1536]{1,0:T(8,128)(2,1)S(1)} %fusion.9), kind=kOutput, calls=%fused_computation.15 | convolution fusion | flops 7264272384 | bytes 18874368 | tf_op jit(solution)/shard_map/cond/branch_1_fun/dot_general | solution.py:468
  735.0 12.1 %add_convert_fusion.3 = bf16[1536,1536]{1,0:T(8,128)(2,1)S(1)} fusion(bf16[1536,1536]{1,0:T(8,128)(2,1)} %fusion.7), kind=kOutput, calls=%fused_computation.20 | convolution fusion | flops 7259553792 | bytes 9437184 | tf_op jit(solution)/shard_map/cond/branch_1_fun/dot_general | solution.py:468
  747.2 10.2 %add_convert_fusion.1.clone.4 = bf16[1536,1536]{1,0:T(8,128)(2,1)} fusion(bf16[1536,1536]{1,0:T(8,128)(2,1)S(1)} %copy-done.56, bf16[1536,1536]{1,0:T(8,128)(2,1)S(1)} %add_convert_fusion.3), kind=kOutput, calls=%fused_computation.18.clone.clone.clone.1 | convolution fusion | flops 7264272384 | bytes 14155776 | tf_op jit(solution)/shard_map/cond/branch_1_fun/dot_general | solution.py:468
  757.4 23.3 %add_convert_fusion = bf16[1536,4096]{1,0:T(8,128)(2,1)} fusion(bf16[1536,4096]{1,0:T(8,128)(2,1)S(1)} %bitcast.402, f32[]{:T(128)S(6)} %div.5, f32[]{:T(128)S(6)} %mul.540, bf16[1536,1536]{1,0:T(8,128)(2,1)} %add_convert_fusion.1.clone.4), kind=kOutput, calls=%fused_computation | convolution fusion | flops 19358810112 | bytes 29884424 | tf_op jit(solution)/shard_map/cond/branch_1_fun/dot_general | solution.py:468
  789.0 136.6 %move_9.1 = (bf16[2,48,4096]{2,1,0:T(8,128)(2,1)}, bf16[1,128,1536]{2,1,0:T(8,128)(2,1)}, bf16[2,48,1536]{2,1,0:T(8,128)(2,1)}, bf16[2,48,768]{2,1,0:T(8,128)(2,1)}) custom-call(bf16[32,48,4096]{2,1,0:T(8,128)(2,1)} %get-tuple-element.142.refs_0_, bf16[32,128,1536]{2,1,0:T(8,128)(2,1)} %get-tuple-element.214.refs_1_, ...), custom_call_target="tpu_custom_call" | custom-call | tf_op jit(solution)/shard_map/move_9/pallas_call | solution.py:421
  (242 shorter events, 132.0 us)
Async XLA Ops:
  0.7 7.8 copy-start.31
  2.2 70.9 %copy-start.21 = (f32[128,48]{0,1:T(8,128)}, f32[128,48]{0,1:T(8,128)S(1)}, u32[]{:S(2)}) copy-start(f32[128,48]{0,1:T(8,128)S(1)} %get-tuple-element.277) | copy-start | bytes 73732
  2.2 70.9 %copy-start.23 = (f32[128,48]{0,1:T(8,128)}, f32[128,48]{0,1:T(8,128)S(1)}, u32[]{:S(2)}) copy-start(f32[128,48]{0,1:T(8,128)S(1)} %get-tuple-element.278) | copy-start | bytes 73732
  79.1 59.3 %copy-start.3 = (bf16[128,1536]{1,0:T(8,128)(2,1)S(1)}, bf16[128,1536]{1,0:T(8,128)(2,1)}, u32[]{:S(2)}) copy-start(bf16[128,1536]{1,0:T(8,128)(2,1)} %refs_0_.2) | copy-start | bytes 1179652
  139.1 197.3 %copy-start.40 = (f32[128]{0:T(128)}, f32[128]{0:T(128)S(1)}, u32[]{:S(2)}) copy-start(f32[128]{0:T(128)S(1)} %get-tuple-element.284) | copy-start | bytes 1540
  335.7 51.1 %copy-start.45 = (f32[128]{0:T(128)}, f32[128]{0:T(128)S(1)}, u32[]{:S(2)}) copy-start(f32[128]{0:T(128)S(1)} %broadcast_multiply_fusion.1) | copy-start | bytes 1540
  465.1 8.4 copy-start.42
  465.1 8.8 copy-start.41
  465.1 8.8 copy-start.46
  468.7 7.7 copy-start.35
  473.8 69.1 %copy-start.47 = (f32[2,48]{1,0:T(2,128)S(1)}, f32[2,48]{1,0:T(2,128)}, u32[]{:S(2)}) copy-start(f32[2,48]{1,0:T(2,128)} %param.35) | copy-start | bytes 1156
  542.9 13.3 %copy-start.8 = (f32[48,4,8,128]{3,2,1,0:T(8,128)S(1)}, f32[48,4,8,128]{3,2,1,0:T(8,128)}, u32[]{:S(2)}) copy-start(f32[48,4,8,128]{3,2,1,0:T(8,128)} %copy.131) | copy-start | bytes 2359300
  543.0 13.3 %copy-start.18 = (f32[48,4096]{1,0:T(8,128)S(1)}, f32[48,4096]{1,0:T(8,128)}, u32[]{:S(2)}) copy-start(f32[48,4096]{1,0:T(8,128)} %param.41) | copy-start | bytes 2359300
  544.7 13.3 %copy-start.16 = (f32[48,1536]{1,0:T(8,128)}, f32[48,1536]{1,0:T(8,128)S(1)}, u32[]{:S(2)}) copy-start(f32[48,1536]{1,0:T(8,128)S(1)} %convert_reduce_fusion.8) | copy-start | bytes 884740
  546.4 11.6 %copy-start.7 = (f32[48,4,8,128]{3,2,1,0:T(8,128)S(1)}, f32[48,4,8,128]{3,2,1,0:T(8,128)}, u32[]{:S(2)}) copy-start(f32[48,4,8,128]{3,2,1,0:T(8,128)} %copy.130) | copy-start | bytes 2359300
  546.8 13.0 %copy-start.17 = (f32[48,1536]{1,0:T(8,128)}, f32[48,1536]{1,0:T(8,128)S(1)}, u32[]{:S(2)}) copy-start(f32[48,1536]{1,0:T(8,128)S(1)} %reshape.473) | copy-start | bytes 884740
  548.1 11.7 %copy-start.26 = (f32[48,768]{1,0:T(8,128)}, f32[48,768]{1,0:T(8,128)S(1)}, u32[]{:S(2)}) copy-start(f32[48,768]{1,0:T(8,128)S(1)} %reshape.474) | copy-start | bytes 442372
  548.1 10.0 %copy-start.19 = (f32[48,4096]{1,0:T(8,128)S(1)}, f32[48,4096]{1,0:T(8,128)}, u32[]{:S(2)}) copy-start(f32[48,4096]{1,0:T(8,128)} %param.40) | copy-start | bytes 2359300
  556.3 82.0 %copy-start.43 = (bf16[2,48]{1,0:T(2,128)(2,1)S(1)}, bf16[2,48]{1,0:T(2,128)(2,1)}, u32[]{:S(2)}) copy-start(bf16[2,48]{1,0:T(2,128)(2,1)} %get-tuple-element.237.refs_0_) | copy-start | bytes 580
  643.5 24.4 %copy-start.2 = (bf16[1536,4096]{1,0:T(8,128)(2,1)}, bf16[1536,4096]{1,0:T(8,128)(2,1)S(1)}, u32[]{:S(2)}) copy-start(bf16[1536,4096]{1,0:T(8,128)(2,1)S(1)} %copy.247) | copy-start | bytes 37748740 | tf_op jit(solution)/shard_map/cond
  735.0 12.1 %copy-start.56 = (bf16[1536,1536]{1,0:T(8,128)(2,1)S(1)}, bf16[1536,1536]{1,0:T(8,128)(2,1)}, u32[]{:S(2)}) copy-start(bf16[1536,1536]{1,0:T(8,128)(2,1)} %add_convert_fusion.2) | copy-start | bytes 14155780 | tf_op jit(solution)/shard_map/cond
  735.0 22.4 %slice-start = ((s8[12582912]{0:T(1024)(128)(4,1)}), s8[4194304]{0:T(1024)(128)(4,1)S(1)}, s32[]{:S(2)}) async-start(s8[12582912]{0:T(1024)(128)(4,1)} %bitcast.401), calls=%async_computation | async-start | bytes 8388608 | tf_op jit(solution)/shard_map/cond
  735.0 22.4 %slice-start.1 = ((s8[12582912]{0:T(1024)(128)(4,1)}), s8[4194304]{0:T(1024)(128)(4,1)S(1)}, s32[]{:S(2)}) async-start(s8[12582912]{0:T(1024)(128)(4,1)} %bitcast.401), calls=%async_computation.1 | async-start | bytes 8388608 | tf_op jit(solution)/shard_map/cond
  747.2 10.2 %slice-start.2 = ((s8[12582912]{0:T(1024)(128)(4,1)}), s8[4194304]{0:T(1024)(128)(4,1)S(1)}, s32[]{:S(2)}) async-start(s8[12582912]{0:T(1024)(128)(4,1)} %bitcast.401), calls=%async_computation.2 | async-start | bytes 8388608 | tf_op jit(solution)/shard_map/cond
  (35 other events, 109.8 us)

commit v2 on v1

--- a/solution.py
+++ b/solution.py
@@ -28,6 +28,11 @@
 MESH = pl.DeviceIdType.MESH
 low_type = jnp.bfloat16
 wide_type = jnp.float32
+
+TILE = 256
+SIDE = D // TILE
+TILE_PAIRS = tuple((i, j) for j in range(SIDE) for i in range(j + 1))
+ATTENTION_PLANE = 3
 
 
 class Place:
@@ -219,6 +224,345 @@
         pltpu.make_async_copy(part, part, pair_recv).wait()
 
 
+class PlaneReduce(Op):
+    def __init__(self, source, fs, kind):
+        super().__init__(source)
+        self.half, self.kind = fs // 2, kind
+
+    def out(self, dp, fs):
+        return jax.ShapeDtypeStruct((1,) + self.source.shape[1:], self.kind)
+
+    def scratch(self):
+        half, block = self.half, self.source.shape[1:]
+        slots = (half,) + block
+        return [pltpu.SemaphoreType.DMA((half,))] * 5 + [
+            pltpu.VMEM(slots, self.source.dtype),
+            pltpu.VMEM(slots, self.source.dtype),
+            pltpu.VMEM(slots, self.source.dtype),
+            pltpu.VMEM(slots, self.source.dtype),
+            pltpu.VMEM(block, self.kind),
+        ]
+
+    def chip(self, place, k):
+        return (place.f // 2) ^ k, lax.rem(place.f, 2)
+
+    def load(self, place, at, k):
+        chip, core = self.chip(place, k)
+        return pltpu.make_async_copy(at[0].at[2 * chip + core], at[2][5].at[k], at[2][0].at[k])
+
+    def pair(self, place, at, k):
+        chip, core = self.chip(place, k)
+        return pltpu.make_async_remote_copy(
+            at[0].at[2 * chip + 1 - core],
+            at[2][6].at[k],
+            at[2][1].at[k],
+            at[2][2].at[k],
+            device_id=(place.z, place.f + 1 - 2 * core),
+            device_id_type=MESH,
+        )
+
+    def hop(self, place, at, k):
+        chip, core = self.chip(place, k)
+        return pltpu.make_async_remote_copy(
+            at[2][7].at[k],
+            at[2][8].at[k],
+            at[2][3].at[k],
+            at[2][4].at[k],
+            device_id=(place.z, 2 * chip + core),
+            device_id_type=MESH,
+        )
+
+    def order(self):
+        return list(reversed(range(self.half)))
+
+    def start(self, place, at):
+        for k in self.order():
+            self.pair(place, at, k).start()
+            self.load(place, at, k).start()
+
+    def combine(self, place, at):
+        mine, got, joint, came, result = at[2][5:10]
+        high = self.source.shape[1]
+        step_rows = 16
+        steps = high // step_rows
+
+        def part(n):
+            return pl.ds(pl.multiple_of(n * step_rows, step_rows), step_rows)
+
+        for k in self.order():
+            self.load(place, at, k).wait()
+            self.pair(place, at, k).wait_recv()
+            if k:
+
+                def add(n, carry, k=k):
+                    total = mine[k, part(n)].astype(wide_type) + got[k, part(n)].astype(wide_type)
+                    joint[k, part(n)] = total.astype(joint.dtype)
+                    return carry
+
+                lax.fori_loop(0, steps, add, 0)
+                self.hop(place, at, k).start()
+        for k in self.order():
+            if k:
+                self.hop(place, at, k).wait_recv()
+
+        def total_of(n, carry):
+            total = mine[0, part(n)].astype(wide_type) + got[0, part(n)].astype(wide_type)
+            for k in range(1, self.half):
+                total = total + came[k, part(n)].astype(wide_type)
+            result[part(n)] = total.astype(result.dtype)
+            return carry
+
+        lax.fori_loop(0, steps, total_of, 0)
+
+    def release(self, place, at):
+        for k in self.order():
+            self.pair(place, at, k).wait_send()
+            if k:
+                self.hop(place, at, k).wait_send()
+
+    def finish(self, place, at):
+        self.combine(place, at)
+        write = pltpu.make_async_copy(at[2][9], at[1].at[0], at[2][0].at[0])
+        write.start()
+        self.release(place, at)
+        write.wait()
+
+
+class PlaneTotal(PlaneReduce):
+    def __init__(self, source, fs):
+        super().__init__(source, fs, source.dtype)
+
+    def out(self, dp, fs):
+        return jax.ShapeDtypeStruct((fs,) + self.source.shape[1:], self.source.dtype)
+
+    def scratch(self):
+        return super().scratch() + [
+            pltpu.SemaphoreType.DMA((self.half,)),
+            pltpu.SemaphoreType.DMA((self.half,)),
+            pltpu.SemaphoreType.DMA((self.half,)),
+            pltpu.SemaphoreType.DMA((self.half,)),
+        ]
+
+    def across(self, place, at, k):
+        chip, core = self.chip(place, k)
+        return pltpu.make_async_remote_copy(
+            at[2][9],
+            at[1].at[place.f],
+            at[2][10].at[k],
+            at[2][11].at[k],
+            device_id=(place.z, 2 * chip + core),
+            device_id_type=MESH,
+        )
+
+    def onward(self, place, at, k):
+        chip, core = self.chip(place, k)
+        block = at[1].at[2 * chip + core]
+        return pltpu.make_async_remote_copy(
+            block if k else at[2][9],
+            block,
+            at[2][12].at[k],
+            at[2][13].at[k],
+            device_id=(place.z, place.f + 1 - 2 * core),
+            device_id_type=MESH,
+        )
+
+    def finish(self, place, at):
+        self.combine(place, at)
+        for k in self.order():
+            if k:
+                self.across(place, at, k).start()
+        self.onward(place, at, 0).start()
+        write = pltpu.make_async_copy(at[2][9], at[1].at[place.f], at[2][0].at[0])
+        write.start()
+        for k in self.order():
+            if k:
+                self.across(place, at, k).wait_recv()
+                self.onward(place, at, k).start()
+        self.release(place, at)
+        write.wait()
+        for k in self.order():
+            if k:
+                self.across(place, at, k).wait_send()
+            self.onward(place, at, k).wait()
+
+
+class ToPlanes(Op):
+    def __init__(self, source, planes):
+        super().__init__(source)
+        self.planes = planes
+
+    def block_shape(self):
+        return self.source.shape[2:]
+
+    def out(self, dp, fs):
+        return jax.ShapeDtypeStruct((dp * fs,) + self.source.shape[2:], self.source.dtype)
+
+    def start(self, place, at):
+        src, dst, _ = at
+        for i, plane in enumerate(self.planes):
+
+            def step(k, carry, i=i, plane=plane):
+                target = lax.rem(place.f + k, place.fs)
+                self.push(at, src.at[i, target], dst.at[place.me], (plane, target))
+                return carry
+
+            lax.fori_loop(1, place.fs, step, 0)
+
+            @pl.when(place.z == plane)
+            def _():
+                self.keep(at, src.at[i, place.f], dst.at[place.me])
+
+            @pl.when(place.z != plane)
+            def _():
+                self.push(at, src.at[i, place.f], dst.at[place.me], (plane, place.f))
+
+    def finish(self, place, at):
+        total = len(self.planes) * place.fs
+        inside = functools.reduce(lambda x, y: x | y, [place.z == p for p in self.planes])
+
+        @pl.when(inside)
+        def _():
+            self.settle(at, total - 1, place.nd - 1)
+
+        @pl.when(jnp.logical_not(inside))
+        def _():
+            self.settle(at, total, 0)
+
+
+class FromPlanes(Op):
+    def __init__(self, source, planes):
+        super().__init__(source)
+        self.planes = planes
+
+    def out(self, dp, fs):
+        return jax.ShapeDtypeStruct((len(self.planes) * fs,) + self.source.shape[1:], self.source.dtype)
+
+    def start(self, place, at):
+        src, dst, _ = at
+        for i, plane in enumerate(self.planes):
+
+            @pl.when(place.z == plane)
+            def _():
+                slot = i * place.fs + place.f
+
+                def step(k, carry):
+                    target = lax.rem(place.me + k, place.nd)
+                    self.push(at, src.at[target], dst.at[slot], place.of(target))
+                    return carry
+
+                lax.fori_loop(1, place.nd, step, 0)
+                self.keep(at, src.at[place.me], dst.at[slot])
+
+    def finish(self, place, at):
+        src, dst, (send_sem, recv_sem, _, _) = at
+        total = len(self.planes) * place.fs
+        inside = functools.reduce(lambda x, y: x | y, [place.z == p for p in self.planes])
+
+        @pl.when(inside)
+        def _():
+            part = src.at[pl.ds(0, place.nd - 1)]
+            pltpu.make_async_copy(part, part, send_sem).wait()
+            self.settle(at, 0, total - 1)
+
+        @pl.when(jnp.logical_not(inside))
+        def _():
+            self.settle(at, 0, total)
+
+
+class ToPlaneOnly(Op):
+    def __init__(self, source, plane):
+        super().__init__(source)
+        self.plane = plane
+
+    def block_shape(self):
+        return self.source.shape
+
+    def out(self, dp, fs):
+        return jax.ShapeDtypeStruct((dp,) + self.source.shape, self.source.dtype)
+
+    def start(self, place, at):
+        src, dst, _ = at
+
+        @pl.when(place.z == self.plane)
+        def _():
+            self.keep(at, src, dst.at[place.z])
+
+        @pl.when(place.z != self.plane)
+        def _():
+            self.push(at, src, dst.at[place.z], (self.plane, place.f))
+
+    def finish(self, place, at):
+        @pl.when(place.z == self.plane)
+        def _():
+            self.settle(at, 0, place.dp - 1)
+
+        @pl.when(place.z != self.plane)
+        def _():
+            self.settle(at, 1, 0)
+
+
+class FromPlaneOnly(Op):
+    def __init__(self, source, plane):
+        super().__init__(source)
+        self.plane = plane
+
+    def out(self, dp, fs):
+        return jax.ShapeDtypeStruct((1,) + self.source.shape[1:], self.source.dtype)
+
+    def start(self, place, at):
+        src, dst, _ = at
+
+        @pl.when(place.z == self.plane)
+        def _():
+            for q in range(place.dp):
+                if q != self.plane:
+                    self.push(at, src.at[q], dst.at[0], (q, place.f))
+            self.keep(at, src.at[self.plane], dst.at[0])
+
+    def finish(self, place, at):
+        src, dst, (send_sem, recv_sem, _, _) = at
+
+        @pl.when(place.z == self.plane)
+        def _():
+            part = src.at[pl.ds(0, place.dp - 1)]
+            pltpu.make_async_copy(part, part, send_sem).wait()
+
+        @pl.when(place.z != self.plane)
+        def _():
+            self.settle(at, 0, 1)
+
+
+class OutToPlane(Op):
+    def out(self, dp, fs):
+        return jax.ShapeDtypeStruct((dp,) + self.source.shape[1:], self.source.dtype)
+
+    def start(self, place, at):
+        src, dst, _ = at
+        for i in range(place.dp):
+            owner = place.f * place.dp + i
+            slot, target = owner // place.fs, lax.rem(owner, place.fs)
+
+            @pl.when(target == place.f)
+            def _():
+                self.keep(at, src.at[i], dst.at[slot])
+
+            @pl.when(target != place.f)
+            def _():
+                self.push(at, src.at[i], dst.at[slot], (place.z, target))
+
+    def finish(self, place, at):
+        first = lax.rem(place.f * place.dp, place.fs)
+        mine = lax.rem(place.f + place.fs - first, place.fs) < place.dp
+
+        @pl.when(mine)
+        def _():
+            self.settle(at, place.dp - 1, place.dp - 1)
+
+        @pl.when(jnp.logical_not(mine))
+        def _():
+            self.settle(at, place.dp, place.dp)
+
+
 class ChainAllToAll(Op):
     def out(self, dp, fs):
         return jax.ShapeDtypeStruct((dp,) + self.source.shape[1:], self.source.dtype)
@@ -272,35 +616,6 @@
             @pl.when(jnp.logical_not(own))
             def _():
                 self.push(at, src, dst.at[slot], (q, column))
-
-    def finish(self, place, at):
-        mine = place.me // place.dp == place.f
-
-        @pl.when(mine)
-        def _():
-            self.settle(at, place.dp - 1, place.dp - 1)
-
-        @pl.when(jnp.logical_not(mine))
-        def _():
-            self.settle(at, place.dp, place.dp)
-
-
-class OutGrads(Op):
-    def out(self, dp, fs):
-        return jax.ShapeDtypeStruct((dp,) + self.source.shape[1:], self.source.dtype)
-
-    def start(self, place, at):
-        src, dst, _ = at
-        for i in range(place.dp):
-            owner = place.f * place.dp + i
-
-            @pl.when(owner == place.me)
-            def _():
-                self.keep(at, src.at[i], dst.at[place.z])
-
-            @pl.when(owner != place.me)
-            def _():
-                self.push(at, src.at[i], dst.at[place.z], place.of(owner))
 
     def finish(self, place, at):
         mine = place.me // place.dp == place.f
@@ -424,7 +739,9 @@
         in_specs=[pl.BlockSpec(memory_space=pl.ANY)] * count,
         out_specs=tuple([pl.BlockSpec(memory_space=pl.ANY)] * count),
         scratch_shapes=sum(scratch, []),
-        compiler_params=pltpu.CompilerParams(collective_id=number, has_side_effects=True),
+        compiler_params=pltpu.CompilerParams(
+            collective_id=number, has_side_effects=True, vmem_limit_bytes=32 << 20
+        ),
         name=f"move_{number}",
     )(*[op.source for op in ops])
 
@@ -476,29 +793,79 @@
     return jnp.einsum("ki,kj->ij", left_side, right_side, preferred_element_type=wide_type)
 
 
-def gram_mixer(gram):
+def mixer_kernel(own_ref, sum_ref, mixer_ref, scale_ref, gram, kept, spare, half):
     a = coeff_a
-    frobenius = jnp.sqrt(jnp.trace(gram))
-    scale = 1.0 / (frobenius + 1e-07)
-    gram_low = (gram * (scale * scale)).astype(low_type)
-    parts = []
-    for number in range(3):
-        square = mul(gram_low, gram_low)
-        part = (coeff_b * gram_low.astype(wide_type) + coeff_c * square).astype(low_type)
-        parts.append(part)
-        if number < 2:
-            half = mul(part, gram_low).astype(low_type)
-            gram_low = (
-                a * a * gram_low.astype(wide_type)
-                + 2.0 * a * half.astype(wide_type)
-                + mul(part, half)
-            ).astype(low_type)
-    first, second, third = parts
-    joint = (
-        a * (first.astype(wide_type) + second.astype(wide_type)) + mul(second, first)
-    ).astype(low_type)
-    mixer = a * a * third.astype(wide_type) + a * joint.astype(wide_type) + mul(third, joint)
-    return scale, mixer.astype(low_type)
+    alone = lax.axis_index("dp") == ATTENTION_PLANE
+
+    def tile_of(number):
+        return jnp.where(alone, own_ref[number], sum_ref[number]).astype(wide_type)
+
+    shape = (TILE, TILE)
+    diagonal = lax.broadcasted_iota(jnp.int32, shape, 0) == lax.broadcasted_iota(jnp.int32, shape, 1)
+    total = jnp.zeros((1, 1), wide_type)
+    for number, (i, j) in enumerate(TILE_PAIRS):
+        if i == j:
+            kept_part = jnp.where(diagonal, tile_of(number), 0.0)
+            total = total + jnp.sum(
+                jnp.sum(kept_part, axis=1, keepdims=True), axis=0, keepdims=True
+            )
+    scale = 1.0 / (jnp.sqrt(total) + 1e-07)
+    scale_ref[...] = jnp.broadcast_to(scale, scale_ref.shape)
+    square = scale * scale
+
+    def span(i):
+        return pl.ds(i * TILE, TILE)
+
+    def put(target, i, j, value):
+        target[span(i), span(j)] = value
+        if i != j:
+            target[span(j), span(i)] = value.T
+
+    for number, (i, j) in enumerate(TILE_PAIRS):
+        put(gram, i, j, (tile_of(number) * square).astype(low_type))
+
+    def product(left, right, target, finish):
+        for i, j in TILE_PAIRS:
+            value = mul(left[span(i), :], right[:, span(j)])
+            put(target, i, j, finish(value, lambda ref: ref[span(i), span(j)].astype(wide_type)).astype(low_type))
+
+    def poly(source, target):
+        product(
+            source, source, target, lambda value, tile: coeff_b * tile(source) + coeff_c * value
+        )
+
+    def step(factor, source, target):
+        product(factor, source, half, lambda value, tile: value)
+        product(
+            factor,
+            half,
+            target,
+            lambda value, tile: a * a * tile(source) + 2.0 * a * tile(half) + value,
+        )
+
+    poly(gram, kept)
+    step(kept, gram, spare)
+    poly(spare, gram)
+    step(gram, spare, mixer_ref)
+    product(gram, kept, half, lambda value, tile: a * (tile(gram) + tile(kept)) + value)
+    poly(mixer_ref, spare)
+    product(
+        spare, half, mixer_ref, lambda value, tile: a * a * tile(spare) + a * tile(half) + value
+    )
+
+
+def gram_mixer(own_tiles, sum_tiles):
+    matrix = jax.ShapeDtypeStruct((D, D), low_type)
+    mixer, scale = pl.pallas_call(
+        mixer_kernel,
+        out_shape=(matrix, jax.ShapeDtypeStruct((8, 128), wide_type)),
+        in_specs=[pl.BlockSpec(memory_space=pltpu.VMEM)] * 2,
+        out_specs=(pl.BlockSpec(memory_space=pltpu.VMEM),) * 2,
+        scratch_shapes=[pltpu.VMEM((D, D), low_type)] * 4,
+        compiler_params=pltpu.CompilerParams(vmem_limit_bytes=44 << 20),
+        name="gram_mixer",
+    )(own_tiles, sum_tiles)
+    return scale[0, 0], mixer
 
 
 def body(
@@ -535,7 +902,6 @@
     repeat = max(1, fs // KV_HEADS)
     group = q_heads // kv_heads
     q_width, kv_width = q_heads * HEAD_DIM, kv_heads * HEAD_DIM
-    go = functools.partial(move, dp=dp, fs=fs)
 
     def run(number, *ops):
         return move(number, dp, fs, *ops)
@@ -604,9 +970,11 @@
     )
     hidden_part = mul(attn_low, out_weight).astype(low_type).reshape(fs, length, D)
 
-    hidden_all, gate_all = run(1, PlaneAllToAll(hidden_part), AllToAll(ff_blocks(w_gate)))
+    hidden_sum, gate_all = run(
+        1, PlaneReduce(hidden_part, fs, wide_type), AllToAll(ff_blocks(w_gate))
+    )
     residual_in = tokens.astype(wide_type)
-    hidden = residual_in + jnp.sum(hidden_all.astype(wide_type), axis=0)
+    hidden = residual_in + hidden_sum[0]
     inverse_two = rms_inverse(hidden)
     normed_two = hidden * inverse_two
     entry_two = (normed_two * gain_rows[1]).astype(low_type)
@@ -634,12 +1002,12 @@
 
     down_out, d_entry_all, grad_down_all = run(
         4,
-        PlaneAllToAll(down_part),
-        PlaneAllToAll(d_entry_part.reshape(fs, length, D)),
+        PlaneReduce(down_part, fs, wide_type),
+        PlaneReduce(d_entry_part.reshape(fs, length, D), fs, wide_type),
         ChainAllToAll(grad_down_part),
     )
-    outputs = (hidden + jnp.sum(down_out.astype(wide_type), axis=0)).astype(low_type)
-    d_entry_two = jnp.sum(d_entry_all.astype(wide_type), axis=0)
+    outputs = (hidden + down_out[0]).astype(low_type)
+    d_entry_two = d_entry_all[0]
     grad_down = jnp.sum(grad_down_all.astype(wide_type), axis=0)
     cot_float = cotangent.astype(wide_type)
     d_hidden = cot_float + rms_back(d_entry_two * gain_rows[1], normed_two, inverse_two)
@@ -679,8 +1047,13 @@
     grad_qkv_part = mul_at(entry_one, d_qkv).astype(low_type).reshape(nd, rows, qkv_width)
     d_first_part = mul_bt(d_qkv, qkv_weight).astype(low_type).reshape(fs, length, D)
 
-    d_first_all, grad_up_all = run(6, PlaneAllToAll(d_first_part), AllToAll(grad_up_part))
-    d_entry_one = jnp.sum(d_first_all.astype(wide_type), axis=0)
+    d_first_sum, grad_up_all, grad_out_plane = run(
+        6,
+        PlaneReduce(d_first_part, fs, wide_type),
+        AllToAll(grad_up_part),
+        OutToPlane(grad_out_part),
+    )
+    d_entry_one = d_first_sum[0]
     inverse_one = rms_inverse(residual_in)
     normed_one = residual_in * inverse_one
     grad_tokens = d_hidden + rms_back(d_entry_one * gain_rows[0], normed_one, inverse_one)
@@ -691,7 +1064,7 @@
     )
 
     grad_qkv_all, grad_out_all, grad_gain_all = run(
-        7, AllToAll(grad_qkv_part), OutGrads(grad_out_part), AllToAll(grad_gain_part)
+        7, AllToAll(grad_qkv_part), ChainAllToAll(grad_out_plane), AllToAll(grad_gain_part)
     )
 
     def ff_rows_of(blocks):
@@ -733,26 +1106,24 @@
         (grad + beta_moment * now).astype(low_type) for grad, now in zip(summed, new_moments)
     )
 
-    def linear(z_at, f_at):
-        return (z_at % dp) * fs + f_at % fs
-
-    gate_owner, up_owner = linear(1, 0), linear(1, fs - 2)
-    down_owner = linear(2, 2)
-    query_owner, out_owner = linear(2, 4), linear(0, fs - 2)
-    key_owner, value_owner = linear(3, 0), linear(3, 4)
+    gate_plane, up_plane, down_plane = 0, 1, 2
+    query_owner, out_owner, key_owner, value_owner = [
+        ATTENTION_PLANE * fs + n for n in (0, 6, 2, 4)
+    ]
     gain_whole, wide_all, tall_all, square_all, small_all = run(
         8,
         SpreadAll(nesterov[0]),
-        ToOwners(jnp.stack([nesterov[5], nesterov[6]]), (gate_owner, up_owner)),
-        ToOwners(nesterov[7][None], (down_owner,)),
+        ToPlanes(jnp.stack([ff_blocks(nesterov[5]), ff_blocks(nesterov[6])]), (gate_plane, up_plane)),
+        ToPlaneOnly(nesterov[7], down_plane),
         ToOwners(jnp.stack([nesterov[1], nesterov[4]]), (query_owner, out_owner)),
         ToOwners(jnp.stack([nesterov[2], nesterov[3]]), (key_owner, value_owner)),
     )
+    place_z = lax.axis_index("dp")
     role = jnp.where(
-        (me == gate_owner) | (me == up_owner),
+        (place_z == gate_plane) | (place_z == up_plane),
         1,
         jnp.where(
-            me == down_owner,
+            place_z == down_plane,
             2,
             jnp.where(
                 (me == query_owner) | (me == out_owner),
@@ -761,46 +1132,78 @@
             ),
         ),
     )
-
-    def idle_work(wide, tall, square, small):
-        return wide, tall, square, small
-
-    def step_rows(block, scale, mixer):
-        return (
-            coeff_a**3 * scale * block.astype(wide_type) + scale * mul(block, mixer)
-        ).astype(low_type)
-
-    def wide_work(wide, tall, square, small):
-        matrix = wide.reshape(D, FF)
-        scale, mixer = gram_mixer(mul_bt(matrix, matrix))
-        result = coeff_a**3 * scale * matrix.astype(wide_type) + scale * mul(mixer, matrix)
-        return result.astype(low_type).reshape(wide.shape), tall, square, small
+    tile_slots = -(-len(TILE_PAIRS) // fs)
+    packed = (fs * tile_slots, TILE, TILE)
+
+    def tiles_of(gram):
+        side = gram.shape[0] // TILE
+        blank = jnp.zeros((TILE, TILE), low_type)
+        tiles = [
+            gram[i * TILE : (i + 1) * TILE, j * TILE : (j + 1) * TILE].astype(low_type)
+            if j < side
+            else blank
+            for i, j in TILE_PAIRS
+        ]
+        return jnp.stack(tiles + [blank] * (packed[0] - len(tiles)))
+
+    def gram_of_rows(blocks, width):
+        matrix = blocks.reshape(-1, width)
+        return tiles_of(mul_at(matrix, matrix))
+
+    def gram_of_columns(blocks):
+        matrix = blocks.reshape(D, ff_part)
+        return tiles_of(mul_bt(matrix, matrix))
+
+    own_tiles = lax.switch(
+        role,
+        [
+            lambda wide, tall, square, small: jnp.zeros(packed, low_type),
+            lambda wide, tall, square, small: gram_of_columns(wide),
+            lambda wide, tall, square, small: gram_of_rows(tall, D),
+            lambda wide, tall, square, small: gram_of_rows(square, D),
+            lambda wide, tall, square, small: gram_of_rows(small, KVW),
+        ],
+        wide_all,
+        tall_all,
+        square_all,
+        small_all,
+    )
+    (sum_tiles,) = run(9, PlaneTotal(own_tiles.reshape(fs, tile_slots * TILE, TILE), fs))
+    scale, mixer = gram_mixer(own_tiles, sum_tiles.reshape(packed))
+
+    def finished(matrix, product):
+        return (scale * (coeff_a**3 * matrix.astype(wide_type) + product)).astype(low_type)
+
+    def columns_work(wide, tall, square, small):
+        matrix = wide.reshape(D, ff_part)
+        return finished(matrix, mul(mixer, matrix)).reshape(wide.shape), tall, square, small
 
     def rows_work(slot, width):
         def work(*blocks):
             blocks = list(blocks)
             matrix = blocks[slot].reshape(-1, width)
-            scale, mixer = gram_mixer(mul_at(matrix, matrix))
-            blocks[slot] = step_rows(matrix, scale, mixer).reshape(blocks[slot].shape)
+            product = mul(matrix, mixer[:width, :width])
+            blocks[slot] = finished(matrix, product).reshape(blocks[slot].shape)
             return tuple(blocks)
 
         return work
 
     wide_all, tall_all, square_all, small_all = lax.switch(
         role,
-        [idle_work, wide_work, rows_work(1, D), rows_work(2, D), rows_work(3, KVW)],
+        [lambda *blocks: blocks, columns_work, rows_work(1, D), rows_work(2, D), rows_work(3, KVW)],
         wide_all,
         tall_all,
         square_all,
         small_all,
     )
     wide_new, tall_new, square_new, small_new = run(
-        9,
-        FromOwners(wide_all, (gate_owner, up_owner)),
-        FromOwners(tall_all, (down_owner,)),
+        10,
+        FromPlanes(wide_all, (gate_plane, up_plane)),
+        FromPlaneOnly(tall_all, down_plane),
         FromOwners(square_all, (query_owner, out_owner)),
         FromOwners(small_all, (key_owner, value_owner)),
     )
+    wide_new = wide_new.reshape(2, fs, rows, dp, ff_rows).transpose(0, 2, 3, 1, 4).reshape(2, rows, FF)
     gain_dir = gain_whole.transpose(1, 0, 2).reshape(2, D).astype(wide_type)
     gain_scale = lax.rsqrt(jnp.mean(gain_dir * gain_dir, axis=-1, keepdims=True) + 1e-06)
     updates = [-rate_gain * nesterov[0].astype(wide_type) * gain_scale]

time: 945 us -> 705 us (0.75)
  matrix products: 185 us -> 43.4 us
  Pallas kernels: 647 us -> 555 us
  other arithmetic: 61.7 us -> 33.8 us
  local copies, waits for them, and re-layouts: 29.2 us -> 51.5 us
    pallas_call x10 -> x11, Pallas kernels: 647 us -> 511 us  [move(): pl.pallas_call(kernel, out_shape=tuple((op.out(dp, fs) for op in ops)), i...]
    dot_general x15 -> x6, matrix products: 123 us -> 14.6 us  [mul(): return jnp.dot(left_side, right_side, preferred_element_type=wide_type)]
    pallas_call x0 -> x1, Pallas kernels: none -> 44.6 us  [gram_mixer(): pl.pallas_call(mixer_kernel, out_shape=(matrix, jax.ShapeDtypeStruct((8,...]
    dot_general x6, matrix products: 42.9 us -> 13.9 us  [mul_bt(): jnp.einsum('ik,jk->ij', left_side, right_side, preferred_element_type=wid...]
    cond x11 -> x23, local copies, waits for them, and re-layouts: 4.6 us -> 16 us
where the time goes in v2:
time: 705 us; the launch traced here: 695 us
  Pallas kernels  555 us (79%)
  local copies, waits for them, and re-layouts  51.5 us (7%)
  matrix products  43.4 us (6%)
  other arithmetic  33.8 us (5%)
  loops' own time  9.13 us (1%)
    pallas_call x11, Pallas kernels, move(): pl.pallas_call(kernel, out_shape=tuple((op.out(dp, fs) for op in ops)), i...  511 us
    pallas_call x1, Pallas kernels, gram_mixer(): pl.pallas_call(mixer_kernel, out_shape=(matrix, jax.ShapeDtypeStruct((8,...  44.6 us
    cond x23, local copies, waits for them, and re-layouts  16 us
    dot_general x6, matrix products, mul(): return jnp.dot(left_side, right_side, preferred_element_type=wide_type)  14.6 us

profile of v2, /device:TPU:14, one launch (start us, length us, event | category | flops | bytes accessed | tf_op | source)
XLA Modules:
  0.0 695.4 jit_solution(8308544638215409887)
XLA Ops:
  12.2 50.8 %move_0.1 = (bf16[8,128,1536]{2,1,0:T(8,128)(2,1)S(1)}, s32[8,1,128]{2,1,0:T(1,128)S(1)}, bf16[32,48,384]{2,1,0:T(8,128)(2,1)S(1)}, bf16[4,48,1536]{2,1,0:T(8,128)(2,1)S(1)}, bf16[32,2,48]{2,1,0:T(2,128)(2,1)S(1)}) custom-call(bf16[128,1536]{1,0:T(8,128)(2,1)S(1)} %copy-done, s32[8,1,128]{2,1,0:T(1,128)S(1)} %broadcast_in_dim.13.refs_1_, ...), custom_call_target="tpu_custom_call" | custom-call | tf_op jit(solution)/shard_map/move_0/pallas_call | solution.py:736
  68.9 3.2 fusion.75
  78.9 42.8 %move_1.1 = (f32[1,128,1536]{2,1,0:T(8,128)S(1)}, bf16[32,48,512]{2,1,0:T(8,128)(2,1)S(1)}) custom-call(bf16[8,128,1536]{2,1,0:T(8,128)(2,1)S(1)} %bitcast.589, bf16[8,48,512]{2,1,0:T(8,128)(2,1)S(1)} %copy-done.3), custom_call_target="tpu_custom_call" | custom-call | tf_op jit(solution)/shard_map/move_1/pallas_call | solution.py:736
  122.7 44.0 %move_2.1 = (bf16[8,128,1536]{2,1,0:T(8,128)(2,1)S(1)}, bf16[32,48,512]{2,1,0:T(8,128)(2,1)S(1)}) custom-call(bf16[128,1536]{1,0:T(8,128)(2,1)S(1)} %multiply_convert_fusion.7.refs_0_, bf16[8,48,512]{2,1,0:T(8,128)(2,1)S(1)} %copy-done.2), custom_call_target="tpu_custom_call" | custom-call | tf_op jit(solution)/shard_map/move_2/pallas_call | solution.py:736
  170.3 39.5 %move_3.1 = (bf16[8,128,1536]{2,1,0:T(8,128)(2,1)S(1)}, bf16[4,128,1536]{2,1,0:T(8,128)(2,1)S(1)}) custom-call(bf16[128,1536]{1,0:T(8,128)(2,1)S(1)} %copy-done.1, bf16[128,1536]{1,0:T(8,128)(2,1)S(1)} %copy-done.14), custom_call_target="tpu_custom_call" | custom-call | tf_op jit(solution)/shard_map/move_3/pallas_call | solution.py:736
  209.8 2.6 multiply_convert_fusion.3
  214.3 3.0 convolution_convert_fusion.4
  217.3 3.0 convolution_convert_fusion.5
  225.8 44.1 %move_4.1 = (f32[1,128,1536]{2,1,0:T(8,128)S(1)}, f32[1,128,1536]{2,1,0:T(8,128)S(1)}, bf16[4,128,1536]{2,1,0:T(8,128)(2,1)S(1)}) custom-call(bf16[8,128,1536]{2,1,0:T(8,128)(2,1)S(1)} %bitcast.594, bf16[8,128,1536]{2,1,0:T(8,128)(2,1)S(1)} %bitcast.591, bf16[4,128,1536]{2,1,0:T(8,128)(2,1)S(1)} %bitcast.603), custom_call_target="tpu_custom_call" | custom-call | tf_op jit(solution)/shard_map/move_4/pallas_call | solution.py:736
  275.1 41.7 %move_5.1 = (bf16[8,128,1536]{2,1,0:T(8,128)(2,1)S(1)}, bf16[32,48,512]{2,1,0:T(8,128)(2,1)S(1)}) custom-call(bf16[128,1536]{1,0:T(8,128)(2,1)S(1)} %fusion.126.refs_0_, bf16[32,48,512]{2,1,0:T(8,128)(2,1)S(1)} %bitcast.599), custom_call_target="tpu_custom_call" | custom-call | tf_op jit(solution)/shard_map/move_5/pallas_call | solution.py:736
  328.8 2.9 convolution_convert_fusion.7
  333.5 50.0 %move_6.1 = (f32[1,128,1536]{2,1,0:T(8,128)S(1)}, bf16[32,48,512]{2,1,0:T(8,128)(2,1)S(1)}, bf16[4,48,1536]{2,1,0:T(8,128)(2,1)S(1)}) custom-call(bf16[8,128,1536]{2,1,0:T(8,128)(2,1)S(1)} %bitcast.595, bf16[32,48,512]{2,1,0:T(8,128)(2,1)S(1)} %bitcast.600, bf16[4,48,1536]{2,1,0:T(8,128)(2,1)S(1)} %bitcast.596), custom_call_target="tpu_custom_call" | custom-call | tf_op jit(solution)/shard_map/move_6/pallas_call | solution.py:736
  390.6 2.7 fusion.93
  394.8 47.4 %move_7.1 = (bf16[32,48,384]{2,1,0:T(8,128)(2,1)S(1)}, bf16[4,48,1536]{2,1,0:T(8,128)(2,1)S(1)}, f32[32,2,48]{2,1,0:T(2,128)S(1)}) custom-call(bf16[32,48,384]{2,1,0:T(8,128)(2,1)S(1)} %bitcast.604, bf16[4,48,1536]{2,1,0:T(8,128)(2,1)S(1)} %copy-done.13, f32[32,2,48]{2,1,0:T(2,128)S(1)} %maximum_bitcast_fusion.4.refs_2_), custom_call_target="tpu_custom_call" | custom-call | tf_op jit(solution)/shard_map/move_7/pallas_call | solution.py:736
  449.0 2.9 fusion.102
  452.4 2.9 fusion.101
  455.7 41.9 %move_8.1 = (bf16[32,2,48]{2,1,0:T(2,128)(2,1)S(1)}, bf16[32,48,512]{2,1,0:T(8,128)(2,1)}, bf16[4,128,1536]{2,1,0:T(8,128)(2,1)}, bf16[32,48,1536]{2,1,0:T(8,128)(2,1)}, bf16[32,48,768]{2,1,0:T(8,128)(2,1)S(1)}) custom-call(bf16[2,48]{1,0:T(2,128)(2,1)S(1)} %get-tuple-element.213.refs_0_, bf16[2,8,48,512]{3,2,1,0:T(8,128)(2,1)S(1)} %pad_maximum_fusion.refs_1_, ...), custom_call_target="tpu_custom_call" | custom-call | tf_op jit(solution)/shard_map/move_8/pallas_call | solution.py:736
  498.5 28.7 %conditional.2 = (bf16[24,256,256]{2,1,0:T(8,128)(2,1)}) conditional(s32[]{:T(128)} %clamp.4, () %tuple.43, bf16[32,48,512]{2,1,0:T(8,128)(2,1)} %get-tuple-element.176, (bf16[4,128,1536]{2,1,0:T(8,128)(2,1)}) %tuple.49, bf16[32,48,1536]{2,1,0:T(8,128)(2,1)} %get-tuple-element.178, ...), branch_computations={%region_17.18_spmd, %region_18.19_spmd, %region_19.20_spmd, %regio... | conditional | flops 7250116608 | bytes 15335432 | solution.py:1157
  498.5 4.5 convolution_convert_fusion
  527.2 53.8 %move_9.1 = bf16[8,768,256]{2,1,0:T(8,128)(2,1)S(1)} custom-call(bf16[8,768,256]{2,1,0:T(8,128)(2,1)} %bitcast.156.refs_0_), custom_call_target="tpu_custom_call" | custom-call | tf_op jit(solution)/shard_map/move_9/pallas_call | solution.py:736
  581.0 44.6 %gram_mixer.1 = (bf16[1536,1536]{1,0:T(8,128)(2,1)}, f32[8,128]{1,0:T(8,128)S(1)}) custom-call(bf16[24,256,256]{2,1,0:T(8,128)(2,1)} %get-tuple-element.273.own_ref, bf16[24,256,256]{2,1,0:T(8,128)(2,1)S(1)} %bitcast.590), custom_call_target="tpu_custom_call" | custom-call | tf_op jit(solution)/shard_map/gram_mixer/pallas_call | solution.py:859
  626.1 8.4 %conditional.3 = ((bf16[32,48,512]{2,1,0:T(8,128)(2,1)}, bf16[4,128,1536]{2,1,0:T(8,128)(2,1)}, bf16[32,48,1536]{2,1,0:T(8,128)(2,1)}, bf16[32,48,768]{2,1,0:T(8,128)(2,1)S(1)})) conditional(s32[]{:T(128)} %clamp.4, (bf16[32,48,512]{2,1,0:T(8,128)(2,1)}, bf16[4,128,1536]{2,1,0:T(8,128)(2,1)}, ...), branch_computations={%region_22.23_spmd, %region_23.24_spmd, %region_24.25_spmd, %regio... | conditional | flops 7259553792 | bytes 42467400 | solution.py:1191
  627.5 6.8 fusion.70
  634.5 54.5 %move_10.1 = (bf16[16,48,512]{2,1,0:T(8,128)(2,1)S(1)}, bf16[1,128,1536]{2,1,0:T(8,128)(2,1)S(1)}, bf16[2,48,1536]{2,1,0:T(8,128)(2,1)S(1)}, bf16[2,48,768]{2,1,0:T(8,128)(2,1)S(1)}) custom-call(bf16[32,48,512]{2,1,0:T(8,128)(2,1)} %get-tuple-element.182.refs_0_, bf16[4,128,1536]{2,1,0:T(8,128)(2,1)} %get-tuple-element.183.refs_1_, ...), custom_call_target="tpu_custom_call" | custom-call | tf_op jit(solution)/shard_map/move_10/pallas_call | solution.py:736
  (278 shorter events, 94.2 us)
Async XLA Ops:
  0.7 8.5 %copy-start.46 = (bf16[48,4096]{1,0:T(8,128)(2,1)S(1)}, bf16[48,4096]{1,0:T(8,128)(2,1)}, u32[]{:S(2)}) copy-start(bf16[48,4096]{1,0:T(8,128)(2,1)} %param.38) | copy-start | bytes 1179652
  4.9 5.4 copy-start
  4.9 5.4 copy-start.16
  78.9 43.8 %copy-start.2 = (bf16[8,48,512]{2,1,0:T(8,128)(2,1)S(1)}, bf16[8,48,512]{2,1,0:T(8,128)(2,1)}, u32[]{:S(2)}) copy-start(bf16[8,48,512]{2,1,0:T(8,128)(2,1)} %reshape.478.refs_1_) | copy-start | bytes 1179652
  121.9 148.8 %copy-start.20 = (f32[128,1536]{1,0:T(8,128)}, f32[128,1536]{1,0:T(8,128)S(1)}, u32[]{:S(2)}) copy-start(f32[128,1536]{1,0:T(8,128)S(1)} %get-tuple-element.216) | copy-start | bytes 2359300
  122.5 149.2 %copy-start.59 = (f32[128]{0:T(128)}, f32[128]{0:T(128)S(1)}, u32[]{:S(2)}) copy-start(f32[128]{0:T(128)S(1)} %get-tuple-element.252) | copy-start | bytes 1540
  273.2 43.6 %copy-start.11 = (bf16[4,48,1536]{2,1,0:T(8,128)(2,1)S(1)}, bf16[4,48,1536]{2,1,0:T(8,128)(2,1)}, u32[]{:S(2)}) copy-start(bf16[4,48,1536]{2,1,0:T(8,128)(2,1)} %copy-done.9) | copy-start | bytes 1769476
  322.2 3.2 copy-start.24
  322.2 3.2 copy-start.47
  322.2 3.2 copy-start.51
  322.2 3.2 copy-start.55
  322.2 3.2 copy-start.57
  384.4 5.9 copy-start.61
  384.4 6.2 copy-start.60
  384.4 6.2 copy-start.64
  390.3 3.2 copy-start.13
  390.6 51.8 %copy-start.65 = (f32[2,48]{1,0:T(2,128)S(1)}, f32[2,48]{1,0:T(2,128)}, u32[]{:S(2)}) copy-start(f32[2,48]{1,0:T(2,128)} %param.40) | copy-start | bytes 1156
  443.1 4.2 copy-start.29
  443.1 3.4 copy-start.48
  443.5 5.5 copy-start.40
  443.5 5.5 copy-start.26
  443.9 8.0 %copy-start.30 = (f32[48,1536]{1,0:T(8,128)}, f32[48,1536]{1,0:T(8,128)S(1)}, u32[]{:S(2)}) copy-start(f32[48,1536]{1,0:T(8,128)S(1)} %reshape.499) | copy-start | bytes 884740
  444.2 4.8 copy-start.41
  449.0 3.4 copy-start.25
  (42 other events, 62.9 us)
